TPU v7x, 128 devices: a whole 4x4x4 slice. The times are simulated.
128 devices in a mesh: col: 2 (over core), row: 64 (over z, y, x).
Axes of the slice: x: 4, y: 4, z: 4, core: 2. Of those that a mesh axis runs over, the one named last changes fastest.
Arguments:
- inter_mask: int32 [65536, 4096], P('row', 'col')
- emb_user: bfloat16 [65536, 64], P(('row', 'col'))
- emb_item: bfloat16 [4096, 64], P(('col', 'row'))
- triples: int32 [128, 3], replicated
Outputs:
- output 1: bfloat16 [65536, 64], P(('row', 'col'))
- output 2: bfloat16 [4096, 64], P(('col', 'row'))
- output 3: float32 [], replicated
All inputs are finite; a program needn't handle non-finite values.
Results may differ from a plain program's by a relative error of at most 0.00519882.
Values are sent between devices in bfloat16 or wider.
A program may use at most 1 GiB of HBM per device.

v0:
```python
import jax
import jax.numpy as jnp
from jax import lax
from jax.sharding import PartitionSpec as P, NamedSharding

LAYERS = 3


def lookup_rows(emb_table, row_ids, row_base):
    local_ids = row_ids - row_base
    inside = (local_ids >= 0) & (local_ids < emb_table.shape[0])
    got_rows = jnp.take(emb_table, jnp.clip(local_ids, 0, emb_table.shape[0] - 1), axis=0).astype(jnp.float32)
    return jnp.where(inside[:, None], got_rows, 0.0)


def solution(mesh):
    row_count = mesh.shape["row"]
    col_count = mesh.shape["col"]

    def local_prog(mask_blk, user_shard, item_shard, triples):
        row_idx = lax.axis_index("row")
        col_idx = lax.axis_index("col")
        deg_user = jnp.maximum(lax.psum(jnp.sum(mask_blk, axis=1), "col"), 1)
        deg_item = jnp.maximum(lax.psum(jnp.sum(mask_blk, axis=0), "row"), 1)
        scale_user = lax.rsqrt(deg_user.astype(jnp.float32))
        scale_item = lax.rsqrt(deg_item.astype(jnp.float32))
        norm_adj = (mask_blk.astype(jnp.float32) * scale_user[:, None] * scale_item[None, :]).astype(jnp.bfloat16)
        layer_user = user_shard
        layer_item = item_shard
        total_user = user_shard.astype(jnp.float32)
        total_item = item_shard.astype(jnp.float32)
        for layer_idx in range(LAYERS):
            item_panel = lax.all_gather(layer_item, "row", axis=0, tiled=True)
            user_part = jnp.dot(norm_adj, item_panel, preferred_element_type=jnp.float32)
            next_user = lax.psum_scatter(user_part, "col", scatter_dimension=0, tiled=True).astype(jnp.bfloat16)
            user_panel = lax.all_gather(layer_user, "col", axis=0, tiled=True)
            item_part = lax.dot_general(norm_adj, user_panel, (((0,), (0,)), ((), ())), preferred_element_type=jnp.float32)
            next_item = lax.psum_scatter(item_part, "row", scatter_dimension=0, tiled=True).astype(jnp.bfloat16)
            total_user = total_user + next_user.astype(jnp.float32)
            total_item = total_item + next_item.astype(jnp.float32)
            layer_user = next_user
            layer_item = next_item
        out_user = (total_user / (LAYERS + 1)).astype(jnp.bfloat16)
        out_item = (total_item / (LAYERS + 1)).astype(jnp.bfloat16)
        user_base = (row_idx * col_count + col_idx) * out_user.shape[0]
        item_base = (col_idx * row_count + row_idx) * out_item.shape[0]
        trip_count = triples.shape[0]
        picked = jnp.concatenate([lookup_rows(out_user, triples[:, 0], user_base), lookup_rows(out_item, triples[:, 1], item_base), lookup_rows(out_item, triples[:, 2], item_base)], axis=0)
        picked = lax.psum(picked, ("row", "col"))
        user_vec = picked[:trip_count]
        pos_vec = picked[trip_count:2 * trip_count]
        neg_vec = picked[2 * trip_count:]
        margin = jnp.sum(user_vec * pos_vec, axis=1) - jnp.sum(user_vec * neg_vec, axis=1)
        bpr_loss = jnp.mean(jax.nn.softplus(-margin))
        return out_user, out_item, bpr_loss

    return jax.shard_map(local_prog, mesh=mesh, in_specs=(P("row", "col"), P(("row", "col"), None), P(("col", "row"), None), P(None, None)), out_specs=(P(("row", "col"), None), P(("col", "row"), None), P()), check_vma=False)
```

profile of v0, /device:TPU:1, one launch (start us, length us, event | category | flops | bytes accessed | tf_op | source)
XLA Modules:
  0.0 1640.7 jit_solution(14677269286440349578)
XLA Ops:
  7.2 4.0 fusion.3
  11.2 21.2 %psum.22 = s32[2048]{0:T(1024)S(1)} all-reduce(s32[2048]{0:T(1024)S(1)} %get-tuple-element.5), channel_id=1, replica_groups=mesh['col'=2,'row'=64] {'row'}, use_global_device_ids=true, to_apply=%region_3.0 | all-reduce | flops 2048 | bytes 16384 | tf_op jit(solution)/shard_map/psum | solution.py:24
  32.4 7.4 psum.21
  39.9 1.9 all_gather.19
  41.8 4.4 multiply_convert_fusion
  46.2 1.9 copy-done
  48.1 2.3 fusion.5
  50.5 146.4 %all_gather.18 = bf16[2048,64]{1,0:T(8,128)(2,1)S(1)} all-gather(bf16[32,64]{1,0:T(8,128)(2,1)S(1)} %copy-done.7), channel_id=1, replica_groups=mesh['col'=2,'row'=64] {'row'}, dimensions={0}, use_global_device_ids=true | all-gather | bytes 266240 | tf_op jit(solution)/shard_map/all_gather | solution.py:33
  196.8 4.3 fusion.4
  201.2 147.3 %reduce-scatter.9.cloned.1.call-done = f32[32,64]{1,0:T(8,128)} async-done(((f32[2048,64]{1,0:T(8,128)}), f32[32,64]{1,0:T(8,128)}) %reduce-scatter.9.cloned.1.call-update) | async-done | bytes 8208 | tf_op jit(solution)/shard_map/reduce_scatter | solution.py:38
  348.5 0.7 convert_element_type.76
  349.3 145.5 %all_gather.20 = bf16[2048,64]{1,0:T(8,128)(2,1)S(1)} all-gather(bf16[32,64]{1,0:T(8,128)(2,1)S(1)} %convert_element_type.76), channel_id=1, replica_groups=mesh['col'=2,'row'=64] {'row'}, dimensions={0}, use_global_device_ids=true | all-gather | bytes 266240 | tf_op jit(solution)/shard_map/all_gather | solution.py:33
  494.7 4.3 fusion.6
  499.1 0.9 convert_element_type.74
  500.0 80.8 %all_gather.21 = bf16[1024,64]{0,1:T(8,128)(2,1)S(1)} all-gather(bf16[512,64]{0,1:T(8,128)(2,1)S(1)} %convert_element_type.74), channel_id=1, replica_groups=mesh['col'=2,'row'=64] {'col'}, dimensions={0}, use_global_device_ids=true | all-gather | bytes 196608 | tf_op jit(solution)/shard_map/all_gather | solution.py:36
  580.8 4.5 fusion.7
  585.4 0.9 convert_element_type.77
  586.3 1.9 all_gather.23
  588.2 4.5 fusion.9
  592.8 295.3 %reduce-scatter.13.cloned.1.call-done = f32[32,64]{1,0:T(8,128)} async-done(((f32[2048,64]{1,0:T(8,128)}), f32[32,64]{1,0:T(8,128)}) %reduce-scatter.13.cloned.1.call-update) | async-done | bytes 8208 | tf_op jit(solution)/shard_map/reduce_scatter | solution.py:38
  888.1 352.7 %reduce-scatter.17.cloned.1.call-done = f32[32,64]{1,0:T(8,128)} async-done(((f32[2048,64]{1,0:T(8,128)}), f32[32,64]{1,0:T(8,128)}) %reduce-scatter.17.cloned.1.call-update) | async-done | bytes 8208 | tf_op jit(solution)/shard_map/reduce_scatter | solution.py:38
  1240.8 0.7 multiply_convert_fusion.2
  1241.6 146.3 %all_gather.22 = bf16[2048,64]{1,0:T(8,128)(2,1)S(1)} all-gather(bf16[32,64]{1,0:T(8,128)(2,1)S(1)} %get-tuple-element.15), channel_id=1, replica_groups=mesh['col'=2,'row'=64] {'row'}, dimensions={0}, use_global_device_ids=true | all-gather | bytes 266240 | tf_op jit(solution)/shard_map/all_gather | solution.py:33
  1387.9 4.3 fusion.8
  1392.3 0.7 gather_fusion.1
  1393.0 0.7 gather_fusion.2
  1393.8 84.2 %reduce-scatter.15.cloned.1.call-done = f32[512,64]{0,1:T(8,128)} async-done(((f32[1024,64]{0,1:T(8,128)}), f32[512,64]{0,1:T(8,128)}) %reduce-scatter.15.cloned.1.call-update) | async-done | bytes 131088 | tf_op jit(solution)/shard_map/reduce_scatter | solution.py:35
  1478.0 0.9 multiply_convert_fusion.1
  1479.1 0.7 gather_fusion
  1479.9 0.7 pad_maximum_fusion
  1480.6 149.8 %all-reduce.2.cloned.1.call-done = f32[384,64]{1,0:T(8,128)} async-done(((f32[384,64]{1,0:T(8,128)}), f32[384,64]{1,0:T(8,128)}) %all-reduce.2.cloned.1.call-update) | async-done | bytes 98320 | tf_op jit(solution)/shard_map/psum | solution.py:49
  1630.4 1.0 fusion
  (44 shorter events, 1.5 us)
Async XLA Ops:
  7.2 32.7 %copy-start.4 = (bf16[512,64]{0,1:T(8,128)(2,1)S(1)}, bf16[512,64]{0,1:T(8,128)(2,1)}, u32[]{:S(2)}) copy-start(bf16[512,64]{0,1:T(8,128)(2,1)} %param.7) | copy-start | bytes 196612
  7.2 341.4 %reduce-scatter.9.cloned.1.call-start = ((), (), s32[]{:S(2)}) async-start(), calls=%async_computation.7 | async-start | bytes 1064960 | tf_op jit(solution)/shard_map/reduce_scatter | solution.py:38
  46.2 1.9 copy-start
  48.1 2.4 copy-start.7
  50.4 448.7 %reduce-scatter.7.cloned.1.call-start = ((), (), s32[]{:S(2)}) async-start(), calls=%async_computation.6 | async-start | bytes 393216 | tf_op jit(solution)/shard_map/reduce_scatter | solution.py:35
  201.2 384.2 %reduce-scatter.11.cloned.1.call-start = ((), (), s32[]{:S(2)}) async-start(), calls=%async_computation.8 | async-start | bytes 393216 | tf_op jit(solution)/shard_map/reduce_scatter | solution.py:35
  499.0 389.1 %reduce-scatter.13.cloned.1.call-start = ((), (), s32[]{:S(2)}) async-start(), calls=%async_computation.9 | async-start | bytes 1064960 | tf_op jit(solution)/shard_map/reduce_scatter | solution.py:38
  585.3 7.5 copy-start.8
  585.3 655.5 %copy-start.6 = (f32[32,64]{1,0:T(8,128)S(1)}, f32[32,64]{1,0:T(8,128)}, u32[]{:S(2)}) copy-start(f32[32,64]{1,0:T(8,128)} %reduce-scatter.9.cloned.1.call-done) | copy-start | bytes 24580
  585.3 655.5 %reduce-scatter.17.cloned.1.call-start = ((), (), s32[]{:S(2)}) async-start(), calls=%async_computation.11 | async-start | bytes 1064960 | tf_op jit(solution)/shard_map/reduce_scatter | solution.py:38
  592.7 885.3 %copy-start.2 = (f32[512,64]{0,1:T(8,128)S(1)}, f32[512,64]{0,1:T(8,128)}, u32[]{:S(2)}) copy-start(f32[512,64]{0,1:T(8,128)} %reduce-scatter.7.cloned.1.call-done) | copy-start | bytes 393220
  592.7 885.3 %copy-start.3 = (f32[512,64]{0,1:T(8,128)S(1)}, f32[512,64]{0,1:T(8,128)}, u32[]{:S(2)}) copy-start(f32[512,64]{0,1:T(8,128)} %reduce-scatter.11.cloned.1.call-done) | copy-start | bytes 393220
  592.7 885.3 %reduce-scatter.15.cloned.1.call-start = ((), (), s32[]{:S(2)}) async-start(), calls=%async_computation.10 | async-start | bytes 393216 | tf_op jit(solution)/shard_map/reduce_scatter | solution.py:35
  1241.6 389.9 %copy-start.1 = (bf16[32,64]{1,0:T(8,128)(2,1)}, bf16[32,64]{1,0:T(8,128)(2,1)S(1)}, u32[]{:S(2)}) copy-start(bf16[32,64]{1,0:T(8,128)(2,1)S(1)} %get-tuple-element.14) | copy-start | bytes 12292
  1392.2 238.2 %all-reduce.2.cloned.1.call-start = ((), (), s32[]{:S(2)}) async-start(), calls=%async_computation.12 | async-start | bytes 393216 | tf_op jit(solution)/shard_map/psum | solution.py:49
  1479.0 153.8 %copy-start.5 = (bf16[512,64]{0,1:T(8,128)(2,1)}, bf16[512,64]{0,1:T(8,128)(2,1)S(1)}, u32[]{:S(2)}) copy-start(bf16[512,64]{0,1:T(8,128)(2,1)S(1)} %multiply_convert_fusion.1) | copy-start | bytes 196612
Sparse Core Ops, SparseCore 0:
  50.5 297.9 reduce-scatter.8
  350.9 56.8 reduce-scatter.6
  499.2 83.9 reduce-scatter.10
  585.4 302.6 reduce-scatter.12
  890.3 350.4 reduce-scatter.16
  1392.3 85.6 reduce-scatter.14
  1482.7 147.6 all-reduce.1
where the time goes:
time: 1640 us
  waiting for transfers between devices  1030 us (63%)
  blocking collectives  551 us (34%)
  matrix products  24.1 us (1%)
    reduce_scatter x3, waiting for transfers between devices, local_prog(): lax.psum_scatter(item_part, 'row', scatter_dimension=0, tiled=True)  795 us
    all_gather x3, blocking collectives, local_prog(): item_panel = lax.all_gather(layer_item, 'row', axis=0, tiled=True)  438 us
    psum x1, waiting for transfers between devices, local_prog(): picked = lax.psum(picked, ('row', 'col'))  150 us
    all_gather x3, blocking collectives, local_prog(): user_panel = lax.all_gather(layer_user, 'col', axis=0, tiled=True)  84.6 us
    reduce_scatter x3, waiting for transfers between devices, local_prog(): lax.psum_scatter(user_part, 'col', scatter_dimension=0, tiled=True)  84.2 us
  transfers between devices with their start and end apart: 7, of which 5 were waited for; matrix products, arithmetic and copies ran while one was open for 1% of the time, Pallas kernels for 0%

commit v1 on v0

v1 whole, which is shorter than its diff:
```python
import jax
import jax.numpy as jnp
from jax import lax
from jax.experimental import pallas as pl
from jax.experimental.pallas import tpu as pltpu
from jax.sharding import PartitionSpec as P

F32 = jnp.float32
BF16 = jnp.bfloat16
LANES = 128


def solution(mesh):
    rows_n = mesh.shape["row"]
    side = round(rows_n ** (1 / 3))
    plane = side * side

    def kernel(m_hbm, eu_hbm, ei_hbm, trip_hbm, ou_hbm, oi_hbm, loss_hbm,
               m32, a, at, cacc, trip, deg, usum, suc, svr, svc, e0, e0d, eup, eu0,
               up1, ur1, part, r12, panel, up3, ur3, eu23, eud, p3, r3, outd, outu, outi,
               ea, ear1, ea1, ear2, xs, xd, lossv,
               m_sem, in_sem, out_sem,
               deg_s, deg_r, e0_s, e0_r, eu0_s, eu0_r, us_s, us_r, u1_s, u1_r, rs_s, rs_r,
               ag_s, ag_r, u3_s, u3_r, r3_s, r3_r, ea1_s, ea1_r, ea2_s, ea2_r, xs_s, xs_r, xd_s, xd_r):
        me = lax.axis_index("row")
        col = lax.axis_index("col")
        mx = me % side
        my = (me // side) % side
        mz = me // plane
        users, items = a.shape
        half = users // 2
        shard = items // rows_n
        ublk = users // LANES
        iblk = items // LANES

        def peer(o):
            px = (mx + o % side) % side
            py = (my + (o // side) % side) % side
            pz = (mz + o // plane) % side
            return px + side * py + plane * pz

        def dup_lo(v):
            lane = lax.broadcasted_iota(jnp.int32, v.shape, v.ndim - 1)
            return jnp.where(lane < 64, v, pltpu.roll(v, 64, v.ndim - 1))

        def dup_hi(v):
            lane = lax.broadcasted_iota(jnp.int32, v.shape, v.ndim - 1)
            return jnp.where(lane < 64, pltpu.roll(v, 64, v.ndim - 1), v)

        def each_peer(fn):
            def body(o, carry):
                fn(peer(o))
                return carry
            lax.fori_loop(1, rows_n, body, 0)

        def send(src, dst, ssem, rsem, where):
            pltpu.make_async_remote_copy(src_ref=src, dst_ref=dst, send_sem=ssem, recv_sem=rsem,
                                         device_id=where).start()

        def wait_bytes(ref, sem):
            pltpu.make_async_copy(ref, ref, sem).wait()

        m_copies = []
        for b in range(ublk):
            blk = pl.ds(b * LANES, LANES)
            m_copies.append(pltpu.make_async_copy(m_hbm.at[blk], m32.at[blk], m_sem.at[b]))
            m_copies[-1].start()
        own_u = pl.ds(pl.multiple_of(col * half, half), half)
        own_i = pl.ds(pl.multiple_of(me * shard, shard), shard)
        c_eu = pltpu.make_async_copy(eu_hbm, eu0.at[own_u], in_sem.at[0])
        c_ei = pltpu.make_async_copy(ei_hbm, e0.at[own_i], in_sem.at[1])
        c_tr = pltpu.make_async_copy(trip_hbm, trip, in_sem.at[2])
        c_eu.start()
        c_ei.start()
        c_tr.start()
        barrier = pltpu.get_barrier_semaphore()
        each_peer(lambda p: pl.semaphore_signal(barrier, inc=1, device_id={"row": p}))
        pl.semaphore_signal(barrier, inc=1, device_id={"col": 1 - col})

        cacc[...] = jnp.zeros_like(cacc)
        for b in range(ublk):
            m_copies[b].wait()

            def colsum(i, carry):
                r = pl.ds(pl.multiple_of(b * LANES + i * 32, 32), 32)
                v = m32[r, :].astype(F32)
                cacc[...] += jnp.sum(v.reshape(4, 8, items), axis=0)
                a[r, :] = v.astype(BF16)
                return carry
            lax.fori_loop(0, LANES // 32, colsum, 0)
        dsum = jnp.sum(cacc[...], axis=0, keepdims=True)
        for i in range(iblk):
            deg[me, i:i + 1, :] = dsum[:, i * LANES:(i + 1) * LANES]
        c_eu.wait()
        c_ei.wait()
        c_tr.wait()
        pl.semaphore_wait(barrier, rows_n)
        each_peer(lambda p: send(deg.at[me], deg.at[me], deg_s, deg_r, {"row": p}))
        each_peer(lambda p: send(e0.at[own_i], e0.at[own_i], e0_s, e0_r, {"row": p}))
        send(eu0.at[own_u], eu0.at[own_u], eu0_s, eu0_r, {"col": 1 - col})

        ones = jnp.ones((items, LANES), BF16)
        for b in range(ublk):
            rsum = jnp.dot(a[b * LANES:(b + 1) * LANES, :], ones, preferred_element_type=F32)
            usum[col, b:b + 1, :] = jnp.transpose(rsum)[0:1, :]
        send(usum.at[col], usum.at[col], us_s, us_r, {"col": 1 - col})

        def flip(i, carry):
            c = pl.ds(pl.multiple_of(i * LANES, LANES), LANES)
            at[c, :] = jnp.transpose(a[:, c])
            return carry
        lax.fori_loop(0, iblk, flip, 0)
        wait_bytes(usum.at[0], us_r)
        su = lax.rsqrt(jnp.maximum(usum[0] + usum[1], 1.0))
        for b in range(ublk):
            suc[b * LANES:(b + 1) * LANES, :] = jnp.transpose(jnp.broadcast_to(su[b:b + 1, :], (LANES, LANES)))
        wait_bytes(eu0.at[pl.ds(0, half)], eu0_r)
        eup[:, 0:64] = eu0[...]
        wait_bytes(e0.at[pl.ds(0, (rows_n - 1) * shard)], e0_r)
        e0d[...] = jnp.concatenate([e0[...], e0[...]], axis=1)

        wait_bytes(deg.at[pl.ds(0, rows_n - 1)], deg_r)
        svr[...] = lax.rsqrt(jnp.maximum(jnp.sum(deg[...], axis=0), 1.0))

        def scale_a(i, carry):
            c = pl.ds(pl.multiple_of(i * LANES, LANES), LANES)
            a[:, c] = (a[:, c].astype(F32) * suc[...] * svr[pl.ds(i, 1), :]).astype(BF16)
            return carry
        lax.fori_loop(0, iblk, scale_a, 0)

        lane = lax.broadcasted_iota(jnp.int32, (half, LANES), 1)
        top = jnp.dot(a[0:half, :], e0d[...], preferred_element_type=F32)
        bot = jnp.dot(a[half:users, :], e0d[...], preferred_element_type=F32)
        up1[...] = jnp.where(lane < 64, top, bot)
        send(up1, ur1, u1_s, u1_r, {"col": 1 - col})

        def scale_at(i, carry):
            r = pl.ds(pl.multiple_of(i * LANES, LANES), LANES)
            sv = jnp.transpose(jnp.broadcast_to(svr[pl.ds(i, 1), :], (LANES, LANES)))
            for b in range(ublk):
                c = slice(b * LANES, (b + 1) * LANES)
                at[r, c] = (at[r, c].astype(F32) * su[b:b + 1, :] * sv).astype(BF16)
            return carry
        lax.fori_loop(0, iblk, scale_at, 0)
        wait_bytes(ur1, u1_r)
        s1 = up1[...] + ur1[...]
        eup[0:half, 64:128] = pltpu.roll(s1, 64, 1)[:, 64:128].astype(BF16)
        eup[half:users, 64:128] = s1[:, 64:128].astype(BF16)

        step = 512

        def mm2(i, carry):
            r = pl.ds(pl.multiple_of(i * step, step), step)
            part[r, :] = jnp.dot(at[r, :], eup[...], preferred_element_type=F32)
            return carry
        lax.fori_loop(0, items // step, mm2, 0)
        r12[me] = part[own_i, :]

        def send_rs(p):
            send(part.at[pl.ds(pl.multiple_of(p * shard, shard), shard)], r12.at[me], rs_s, rs_r, {"row": p})
        each_peer(send_rs)
        wait_bytes(r12.at[pl.ds(0, rows_n - 1)], rs_r)
        panel[own_i, :] = jnp.sum(r12[...], axis=0).astype(BF16)
        each_peer(lambda p: send(panel.at[own_i], panel.at[own_i], ag_s, ag_r, {"row": p}))
        wait_bytes(panel.at[pl.ds(0, (rows_n - 1) * shard)], ag_r)

        quarter = users // 4
        for k in range(4):
            r = slice(k * quarter, (k + 1) * quarter)
            up3[r, :] = jnp.dot(a[r, :], panel[...], preferred_element_type=F32)
            send(up3.at[pl.ds(k * quarter, quarter)], ur3.at[pl.ds(k * quarter, quarter)],
                 u3_s.at[k], u3_r.at[k], {"col": 1 - col})
        for k in range(4):
            r = slice(k * quarter, (k + 1) * quarter)
            wait_bytes(ur3.at[pl.ds(k * quarter, quarter)], u3_r.at[k])
            s = up3[r, :] + ur3[r, :]
            eu23[r, :] = s.astype(BF16)
            eud[r, :] = dup_lo(s).astype(BF16)

        groups = step // shard

        def mm4(i, carry):
            r = pl.ds(pl.multiple_of(i * step, step), step)
            v = jnp.dot(at[r, :], eud[...], preferred_element_type=F32).reshape(groups, shard, LANES)
            lo, hi = v[:, 0:shard // 2, :], v[:, shard // 2:shard, :]
            ln = lax.broadcasted_iota(jnp.int32, lo.shape, 2)
            p3[pl.ds(i * groups, groups)] = jnp.where(ln < 64, lo, hi)
            return carry
        lax.fori_loop(0, items // step, mm4, 0)
        r3[me] = p3[me]
        each_peer(lambda p: send(p3.at[p], r3.at[me], r3_s, r3_r, {"row": p}))

        for k in range(4):
            r = slice(k * quarter, (k + 1) * quarter)
            x = eup[r, :].astype(F32)
            y = eu23[r, :].astype(F32)
            t = x + pltpu.roll(x, 64, 1)
            outd[r, :] = ((t + dup_lo(y) + dup_hi(y)) * 0.25).astype(BF16)
        outu[...] = outd[own_u, 0:64]
        c_ou = pltpu.make_async_copy(outu, ou_hbm, out_sem.at[0])
        c_ou.start()
        trips = trip[...]
        ids = lax.broadcasted_iota(jnp.int32, (trips.shape[0], users), 1) + me * users
        hot = jnp.where(ids == trips[:, 0:1], 1.0, 0.0).astype(BF16)
        picked = jnp.dot(hot, outd[...], preferred_element_type=F32)
        tq = picked.shape[0] // 2
        ln = lax.broadcasted_iota(jnp.int32, (tq, LANES), 1)
        ea[...] = jnp.where(ln < 64, picked[0:tq], picked[tq:2 * tq]).astype(BF16)
        for o in range(1, side):
            send(ea, ear1.at[o - 1], ea1_s.at[o - 1], ea1_r.at[o - 1],
                 {"row": (mx + o) % side + side * my + plane * mz})
        for o in range(1, side):
            wait_bytes(ear1.at[o - 1], ea1_r.at[o - 1])
        ea1[...] = (ea[...].astype(F32) + jnp.sum(ear1[...].astype(F32), axis=0)).astype(BF16)

        def send_ea(o, carry):
            pyz = side * ((my + o % side) % side) + plane * ((mz + o // side) % side)
            send(ea1, ear2.at[o], ea2_s, ea2_r, {"row": mx + pyz})
            return carry
        lax.fori_loop(1, plane, send_ea, 0)
        ear2[0] = ea1[...]
        wait_bytes(ear2.at[pl.ds(0, plane - 1)], ea2_r)
        eav = jnp.sum(ear2[...].astype(F32), axis=0)
        users_v = jnp.concatenate([eav[:, 0:64], pltpu.roll(eav, 64, 1)[:, 0:64]], axis=0).astype(BF16)
        pad = jnp.concatenate([trips, jnp.zeros((trips.shape[0], LANES - 3), jnp.int32)], axis=1).astype(F32)
        tr = jnp.transpose(pad)
        base = (col * items + me * shard).astype(F32)
        rowid = lax.broadcasted_iota(jnp.int32, (shard, LANES), 0).astype(F32) + base
        g = panel[own_i, :].astype(F32)
        e0own = e0d[own_i, :].astype(F32)
        tot = e0own + dup_lo(g) + dup_hi(g)

        wait_bytes(r3.at[pl.ds(0, rows_n - 1)], r3_r)
        s3 = jnp.sum(r3[...], axis=0).astype(BF16).astype(F32)
        e3 = jnp.concatenate([dup_lo(s3), dup_hi(s3)], axis=0)
        oi = ((tot + e3) * 0.25).astype(BF16)
        outi[...] = oi[:, 0:64]
        c_oi = pltpu.make_async_copy(outi, oi_hbm, out_sem.at[1])
        c_oi.start()

        dots = lax.dot_general(oi[:, 0:64], users_v, (((1,), (1,)), ((), ())), preferred_element_type=F32)
        xp = jnp.sum(jnp.where(rowid == tr[1:2, :], dots, 0.0), axis=0, keepdims=True)
        xn = jnp.sum(jnp.where(rowid == tr[2:3, :], dots, 0.0), axis=0, keepdims=True)
        xs[me, 0:1, :] = xp - xn
        line = pl.ds(0, 1)
        each_peer(lambda p: send(xs.at[me, line], xs.at[me, line], xs_s, xs_r, {"row": p}))
        wait_bytes(xs.at[pl.ds(0, rows_n - 1), line], xs_r)
        xd[col, 0:1, :] = jnp.sum(xs[:, 0:1, :], axis=0)
        send(xd.at[col, line], xd.at[col, line], xd_s, xd_r, {"col": 1 - col})
        wait_bytes(xd.at[0, line], xd_r)
        neg = -(xd[0, 0:1, :] + xd[1, 0:1, :])
        sp = jnp.maximum(neg, 0.0) + jnp.log1p(jnp.exp(-jnp.abs(neg)))
        lossv[...] = jnp.sum(sp, axis=1, keepdims=True) * (1.0 / sp.shape[1])
        c_lo = pltpu.make_async_copy(lossv, loss_hbm, out_sem.at[2])
        c_lo.start()

        wait_bytes(deg.at[pl.ds(0, rows_n - 1)], deg_s)
        wait_bytes(e0.at[pl.ds(0, (rows_n - 1) * shard)], e0_s)
        wait_bytes(eu0.at[pl.ds(0, half)], eu0_s)
        wait_bytes(usum.at[0], us_s)
        wait_bytes(up1, u1_s)
        wait_bytes(r12.at[pl.ds(0, rows_n - 1)], rs_s)
        wait_bytes(panel.at[pl.ds(0, (rows_n - 1) * shard)], ag_s)
        for k in range(4):
            wait_bytes(up3.at[pl.ds(k * quarter, quarter)], u3_s.at[k])
        wait_bytes(p3.at[pl.ds(0, rows_n - 1)], r3_s)
        for o in range(1, side):
            wait_bytes(ea, ea1_s.at[o - 1])
        wait_bytes(ear2.at[pl.ds(0, plane - 1)], ea2_s)
        wait_bytes(xs.at[pl.ds(0, rows_n - 1), line], xs_s)
        wait_bytes(xd.at[0, line], xd_s)
        c_ou.wait()
        c_oi.wait()
        c_lo.wait()

    def local_prog(mask_blk, user_shard, item_shard, triples):
        users, items = mask_blk.shape
        half, dim = user_shard.shape
        shard = item_shard.shape[0]
        trips = triples.shape[0]
        V = pltpu.VMEM
        D = pltpu.SemaphoreType.DMA
        scratch = [
            V((users, items), jnp.int32), V((users, items), BF16), V((items, users), BF16),
            V((8, items), F32), V((trips, 3), jnp.int32),
            V((rows_n, items // LANES, LANES), F32), V((2, users // LANES, LANES), F32),
            V((users, LANES), F32), V((items // LANES, LANES), F32), V((items, LANES), F32),
            V((items, dim), BF16), V((items, LANES), BF16), V((users, LANES), BF16), V((users, dim), BF16),
            V((half, LANES), F32), V((half, LANES), F32),
            V((items, LANES), F32), V((rows_n, shard, LANES), F32), V((items, LANES), BF16),
            V((users, LANES), F32), V((users, LANES), F32), V((users, LANES), BF16), V((users, LANES), BF16),
            V((rows_n, shard // 2, LANES), F32), V((rows_n, shard // 2, LANES), F32),
            V((users, LANES), BF16), V((half, dim), BF16), V((shard, dim), BF16),
            V((trips // 2, LANES), BF16), V((side - 1, trips // 2, LANES), BF16),
            V((trips // 2, LANES), BF16), V((plane, trips // 2, LANES), BF16),
            V((rows_n, 8, LANES), F32), V((2, 8, LANES), F32), V((1, 1), F32),
            D((users // LANES,)), D((3,)), D((3,)),
        ] + [D, D] * 7
        scratch += [D((4,)), D((4,)), D, D, D((side - 1,)), D((side - 1,)), D, D, D, D, D, D]
        ANY = pl.BlockSpec(memory_space=pl.ANY)
        out_user, out_item, loss = pl.pallas_call(
            kernel,
            out_shape=(jax.ShapeDtypeStruct((half, dim), BF16), jax.ShapeDtypeStruct((shard, dim), BF16),
                       jax.ShapeDtypeStruct((1, 1), F32)),
            in_specs=[ANY] * 4,
            out_specs=(ANY,) * 3,
            scratch_shapes=scratch,
            compiler_params=pltpu.CompilerParams(collective_id=0, has_side_effects=True,
                                                 vmem_limit_bytes=56 << 20),
        )(mask_blk, user_shard, item_shard, triples)
        return out_user, out_item, loss[0, 0]

    return jax.shard_map(local_prog, mesh=mesh, in_specs=(P("row", "col"), P(("row", "col"), None), P(("col", "row"), None), P(None, None)), out_specs=(P(("row", "col"), None), P(("col", "row"), None), P()), check_vma=False)
```

time: 1640 us -> 98 us (0.06)
  waiting for transfers between devices: 1030 us -> 0 us
  blocking collectives: 551 us -> 0 us
  Pallas kernels: 0 us -> 89.5 us
  matrix products: 24.1 us -> 0 us
    reduce_scatter x6 -> x0, waiting for transfers between devices: 880 us -> none  [the longest x3 795 us: local_prog(): lax.psum_scatter(item_part, 'row', scatter_dimension=0, tiled=True)]
    all_gather x6 -> x0, blocking collectives: 523 us -> none  [the longest x3 438 us: local_prog(): item_panel = lax.all_gather(layer_item, 'row', axis=0, tiled=True)]
    psum x1 -> x0, waiting for transfers between devices: 150 us -> none  [local_prog(): picked = lax.psum(picked, ('row', 'col'))]
    pallas_call x0 -> x1, Pallas kernels: none -> 89.5 us  [local_prog(): pl.pallas_call(kernel, out_shape=(jax.ShapeDtypeStruct((half, dim), BF16)...]
    psum x2 -> x0, blocking collectives: 28.6 us -> none  [the longest x1 21.2 us: local_prog(): deg_item = jnp.maximum(lax.psum(jnp.sum(mask_blk, axis=0), 'row'), 1)]
    dot_general x6 -> x0, matrix products: 24.1 us -> none  [the longest x3 12.9 us: local_prog(): jnp.dot(norm_adj, item_panel, preferred_element_type=jnp.float32)]
  transfers between devices with their start and end apart: 7 -> 0, of which waited for: 5 -> 0; matrix products, arithmetic and copies ran while one was open for 1% -> 0% of each run, Pallas kernels for 0% -> 0%
where the time goes in v1:
time: 98 us; the launch traced here: 97.7 us
  Pallas kernels  89.5 us (91%)
  local copies, waits for them, and re-layouts  5.93 us (6%)
  between operations  2.31 us (2%)
    pallas_call x1, Pallas kernels, local_prog(): pl.pallas_call(kernel, out_shape=(jax.ShapeDtypeStruct((half, dim), BF16)...  89.5 us
    unnamed x4, local copies, waits for them, and re-layouts  5.93 us

profile of v1, /device:TPU:1, one launch (start us, length us, event | category | flops | bytes accessed | tf_op | source)
XLA Modules:
  0.0 97.7 jit_solution(663768524653806541)
XLA Ops:
  0.6 1.4 %copy.8.trip_hbm = s32[128,3]{1,0:T(8,128)} copy(s32[128,3]{0,1:T(4,128)} %param.7) | data formatting | bytes 3072 | tf_op args[3]
  2.0 1.6 %copy.7.eu_hbm = bf16[512,64]{1,0:T(8,128)(2,1)} copy(bf16[512,64]{0,1:T(8,128)(2,1)} %param.5) | data formatting | bytes 131072 | tf_op args[1]
  3.6 89.5 %shard_map.67 = (bf16[512,64]{1,0:T(8,128)(2,1)}, bf16[32,64]{1,0:T(8,128)(2,1)}, f32[1,1]{1,0:T(1,128)}) custom-call(s32[1024,2048]{1,0:T(8,128)} %m_hbm.1, bf16[512,64]{1,0:T(8,128)(2,1)} %copy.7.eu_hbm, bf16[32,64]{1,0:T(8,128)(2,1)} %ei_hbm.1, s32[128,3]{1,0:T(8,128)} %copy.8.trip_hbm), custom_call_target="tpu_custom_call" | custom-call | tf_op jit(solution)/shard_map/pallas_call | solution.py:301
  93.1 1.6 %copy.9 = bf16[512,64]{0,1:T(8,128)(2,1)} copy(bf16[512,64]{1,0:T(8,128)(2,1)} %get-tuple-element.9) | data formatting | bytes 131072
  94.8 1.3 %copy.12 = bf16[32,64]{1,0:T(8,128)(2,1)} copy(bf16[32,64]{1,0:T(8,128)(2,1)} %get-tuple-element.16) | data formatting | bytes 8192

commit v2 on v1

v2 whole, which is shorter than its diff:
```python
import jax
import jax.numpy as jnp
from jax import lax
from jax.experimental import pallas as pl
from jax.experimental.pallas import tpu as pltpu
from jax.sharding import PartitionSpec as P

F32 = jnp.float32
BF16 = jnp.bfloat16
LANES = 128
DIM = 64


def solution(mesh):
    rows_n = mesh.shape["row"]
    side = round(rows_n ** (1 / 3))
    plane = side * side

    def far(d):
        return min(d, side - d)

    offsets = [(dx, dy, dz) for dz in range(side) for dy in range(side) for dx in range(side)]
    offsets = sorted(offsets[1:], key=lambda o: -(far(o[0]) + far(o[1]) + far(o[2])))

    def kernel(m_hbm, eu_hbm, ei_hbm, trip_hbm, ou_hbm, oi_hbm, loss_hbm,
               m32, a, at, cacc, trip, deg, usum, suc, svr, eu0t, ei0, e0p, eu0d, e0d, pan1, pan2,
               up1, ur1, up2, ur2, up3, ur3, eu1d, eu2d, eu3d, q1, q2, q3, r1, r2, r3, g1, g2, outd, outu, outi,
               ea, ear1, ea1, ear2, xs, xd, lossv,
               m_sem, in_sem, out_sem,
               deg_s, deg_r, e0_s, e0_r, eu0_s, eu0_r, us_s, us_r, u1_s, u1_r, u2_s, u2_r, u3_s, u3_r,
               r1_s, r1_r, r2_s, r2_r, r3_s, r3_r, g1_s, g1_r, g2_s, g2_r,
               ea1_s, ea1_r, ea2_s, ea2_r, xs_s, xs_r, xd_s, xd_r):
        me = lax.axis_index("row")
        col = lax.axis_index("col")
        mx = me % side
        my = (me // side) % side
        mz = me // plane
        pxs = [(mx + d) % side for d in range(side)]
        pys = [((my + d) % side) * side for d in range(side)]
        pzs = [((mz + d) % side) * plane for d in range(side)]
        users, items = a.shape
        half = users // 2
        shard = items // rows_n
        hs = shard // 2
        ublk = users // LANES
        iblk = items // LANES
        others = pl.ds(0, rows_n - 1)
        line = pl.ds(0, 1)

        def peer(o):
            return pxs[o[0]] + pys[o[1]] + pzs[o[2]]

        def lo_lanes(v):
            return lax.broadcasted_iota(jnp.int32, v.shape, v.ndim - 1) < DIM

        def dup_lo(v):
            return jnp.where(lo_lanes(v), v, pltpu.roll(v, DIM, v.ndim - 1))

        def dup_hi(v):
            return jnp.where(lo_lanes(v), pltpu.roll(v, DIM, v.ndim - 1), v)

        def send(src, dst, ssem, rsem, where):
            pltpu.make_async_remote_copy(src_ref=src, dst_ref=dst, send_sem=ssem, recv_sem=rsem,
                                         device_id=where).start()

        def wait_bytes(ref, sem):
            pltpu.make_async_copy(ref, ref, sem).wait()

        def spread(ref, ssem, rsem):
            for o in offsets:
                send(ref, ref, ssem, rsem, {"row": peer(o)})

        def unpack(src, dst):
            def body(i, carry):
                v = src[pl.ds(i * plane, plane)].astype(F32)
                both = jnp.concatenate([dup_lo(v), dup_hi(v)], axis=1).astype(BF16)
                dst[pl.ds(pl.multiple_of(i * plane * shard, plane * shard), plane * shard), :] = both.reshape(plane * shard, LANES)
                return carry
            lax.fori_loop(0, rows_n // plane, body, 0)

        m_copies = []
        for b in range(ublk):
            blk = pl.ds(b * LANES, LANES)
            m_copies.append(pltpu.make_async_copy(m_hbm.at[blk], m32.at[blk], m_sem.at[b]))
            m_copies[-1].start()
        c_eu = pltpu.make_async_copy(eu_hbm, eu0t.at[col], in_sem.at[0])
        c_ei = pltpu.make_async_copy(ei_hbm, ei0, in_sem.at[1])
        c_tr = pltpu.make_async_copy(trip_hbm, trip, in_sem.at[2])
        c_eu.start()
        c_ei.start()
        c_tr.start()
        barrier = pltpu.get_barrier_semaphore()
        for o in offsets:
            pl.semaphore_signal(barrier, inc=1, device_id={"row": peer(o)})
        pl.semaphore_signal(barrier, inc=1, device_id={"col": 1 - col})

        cacc[...] = jnp.zeros_like(cacc)
        for b in range(ublk):
            m_copies[b].wait()

            def colsum(i, carry):
                r = pl.ds(pl.multiple_of(b * LANES + i * 32, 32), 32)
                v = m32[r, :].astype(F32)
                cacc[...] += jnp.sum(v.reshape(4, 8, items), axis=0)
                a[r, :] = v.astype(BF16)
                return carry
            lax.fori_loop(0, LANES // 32, colsum, 0)
        dsum = jnp.sum(cacc[...], axis=0, keepdims=True)
        for i in range(iblk):
            deg[me, i:i + 1, :] = dsum[:, i * LANES:(i + 1) * LANES]
        c_eu.wait()
        c_ei.wait()
        c_tr.wait()
        own0 = jnp.concatenate([ei0[...], ei0[...]], axis=1).astype(F32)
        e0p[me] = jnp.where(lo_lanes(own0[0:hs]), own0[0:hs], own0[hs:shard]).astype(BF16)
        pl.semaphore_wait(barrier, rows_n)
        spread(deg.at[me], deg_s, deg_r)
        send(eu0t.at[col], eu0t.at[col], eu0_s, eu0_r, {"col": 1 - col})

        ones = jnp.ones((items, LANES), BF16)
        for b in range(ublk):
            rsum = jnp.dot(a[b * LANES:(b + 1) * LANES, :], ones, preferred_element_type=F32)
            usum[col, b:b + 1, :] = jnp.transpose(rsum)[0:1, :]
        send(usum.at[col], usum.at[col], us_s, us_r, {"col": 1 - col})
        spread(e0p.at[me], e0_s, e0_r)

        def flip(i, carry):
            c = pl.ds(pl.multiple_of(i * LANES, LANES), LANES)
            at[c, :] = jnp.transpose(a[:, c])
            return carry
        lax.fori_loop(0, iblk, flip, 0)
        wait_bytes(usum.at[0], us_r)
        su = lax.rsqrt(jnp.maximum(usum[0] + usum[1], 1.0))
        for b in range(ublk):
            suc[b * LANES:(b + 1) * LANES, :] = jnp.transpose(jnp.broadcast_to(su[b:b + 1, :], (LANES, LANES)))
        wait_bytes(eu0t.at[0], eu0_r)
        for c in range(2):
            t = eu0t[c]
            eu0d[c * half:(c + 1) * half, :] = jnp.transpose(jnp.concatenate([t, t], axis=0))

        wait_bytes(deg.at[others], deg_r)
        svr[...] = lax.rsqrt(jnp.maximum(jnp.sum(deg[...], axis=0), 1.0))

        def scale_at(i, carry):
            r = pl.ds(pl.multiple_of(i * LANES, LANES), LANES)
            sv = jnp.transpose(jnp.broadcast_to(svr[pl.ds(i, 1), :], (LANES, LANES)))
            for b in range(ublk):
                c = slice(b * LANES, (b + 1) * LANES)
                at[r, c] = at[r, c] * (su[b:b + 1, :] * sv).astype(BF16)
            return carry
        lax.fori_loop(0, iblk, scale_at, 0)

        def item_sums(eud, q, r, ssem, rsem):
            step = plane * shard
            for dz in sorted(range(side), key=lambda d: -far(d)):
                z = pzs[dz]
                rows = pl.ds(pl.multiple_of(z * shard, step), step)
                v = jnp.dot(at[rows, :], eud[...], preferred_element_type=F32).reshape(plane, shard, LANES)
                lo, hi = v[:, 0:hs, :], v[:, hs:shard, :]
                q[pl.ds(z, plane)] = jnp.where(lo_lanes(lo), lo, hi)
                for o in offsets:
                    if o[2] == dz:
                        p = peer(o)
                        send(q.at[p], r.at[me], ssem, rsem, {"row": p})
            r[me] = q[me]

        def user_sums(pan, up, ur, ssem, rsem):
            h = half // 2
            for k in range(2):
                lo = jnp.dot(a[k * h:(k + 1) * h, :], pan[...], preferred_element_type=F32)
                hi = jnp.dot(a[half + k * h:half + (k + 1) * h, :], pan[...], preferred_element_type=F32)
                up[k * h:(k + 1) * h, :] = jnp.where(lo_lanes(lo), lo, hi)
                send(up.at[pl.ds(k * h, h)], ur.at[pl.ds(k * h, h)], ssem.at[k], rsem.at[k], {"col": 1 - col})

        def user_rows(up, ur, rsem, eud):
            h = half // 2
            for k in range(2):
                wait_bytes(ur.at[pl.ds(k * h, h)], rsem.at[k])
                s = up[k * h:(k + 1) * h, :] + ur[k * h:(k + 1) * h, :]
                eud[k * h:(k + 1) * h, :] = dup_lo(s).astype(BF16)
                eud[half + k * h:half + (k + 1) * h, :] = dup_hi(s).astype(BF16)

        item_sums(eu0d, q1, r1, r1_s, r1_r)

        def scale_a(i, carry):
            c = pl.ds(pl.multiple_of(i * LANES, LANES), LANES)
            a[:, c] = a[:, c] * (suc[...] * svr[pl.ds(i, 1), :]).astype(BF16)
            return carry
        lax.fori_loop(0, iblk, scale_a, 0)
        wait_bytes(e0p.at[others], e0_r)
        unpack(e0p, e0d)
        user_sums(e0d, up1, ur1, u1_s, u1_r)
        user_rows(up1, ur1, u1_r, eu1d)
        item_sums(eu1d, q2, r2, r2_s, r2_r)
        wait_bytes(r1.at[others], r1_r)
        g1[me] = jnp.sum(r1[...], axis=0).astype(BF16)
        spread(g1.at[me], g1_s, g1_r)
        wait_bytes(r2.at[others], r2_r)
        g2[me] = jnp.sum(r2[...], axis=0).astype(BF16)
        spread(g2.at[me], g2_s, g2_r)
        wait_bytes(g1.at[others], g1_r)
        unpack(g1, pan1)
        user_sums(pan1, up2, ur2, u2_s, u2_r)
        user_rows(up2, ur2, u2_r, eu2d)
        item_sums(eu2d, q3, r3, r3_s, r3_r)
        wait_bytes(g2.at[others], g2_r)
        unpack(g2, pan2)
        user_sums(pan2, up3, ur3, u3_s, u3_r)
        user_rows(up3, ur3, u3_r, eu3d)

        quarter = users // 4
        for k in range(4):
            r = slice(k * quarter, (k + 1) * quarter)
            t = eu0d[r, :].astype(F32) + eu1d[r, :].astype(F32) + eu2d[r, :].astype(F32) + eu3d[r, :].astype(F32)
            outd[r, :] = (t * 0.25).astype(BF16)
        trips = trip[...]
        tn = trips.shape[1]
        ids = lax.broadcasted_iota(jnp.int32, (users, tn), 0) + me * users
        hot = jnp.where(ids == trips[0:1, :], 1.0, 0.0)
        picked = jnp.dot(jnp.transpose(hot).astype(BF16), outd[...], preferred_element_type=F32)
        tq = tn // 2
        ea[...] = jnp.where(lo_lanes(picked[0:tq]), picked[0:tq], picked[tq:tn]).astype(BF16)
        for o in (2, 1, 3):
            send(ea, ear1.at[o - 1], ea1_s.at[o - 1], ea1_r.at[o - 1], {"row": pxs[o] + pys[0] + pzs[0]})
        outu[...] = jnp.transpose(outd[pl.ds(pl.multiple_of(col * half, half), half), :])[0:DIM, :]
        c_ou = pltpu.make_async_copy(outu, ou_hbm, out_sem.at[0])
        c_ou.start()
        for o in range(1, side):
            wait_bytes(ear1.at[o - 1], ea1_r.at[o - 1])
        ea1[...] = (ea[...].astype(F32) + jnp.sum(ear1[...].astype(F32), axis=0)).astype(BF16)
        for o in offsets:
            if o[0] == 0:
                send(ea1, ear2.at[o[1] + side * o[2]], ea2_s, ea2_r, {"row": peer(o)})
        ear2[0] = ea1[...]
        g = g1[me].astype(F32)
        h = g2[me].astype(F32)
        tot = (own0 + jnp.concatenate([dup_lo(g), dup_hi(g)], axis=0)) + jnp.concatenate([dup_lo(h), dup_hi(h)], axis=0)
        rowid = lax.broadcasted_iota(jnp.int32, (shard, LANES), 0) + (col * items + me * shard)
        wait_bytes(r3.at[others], r3_r)
        s3 = jnp.sum(r3[...], axis=0).astype(BF16).astype(F32)
        oi = ((tot + jnp.concatenate([dup_lo(s3), dup_hi(s3)], axis=0)) * 0.25).astype(BF16)
        outi[...] = oi[:, 0:DIM]
        c_oi = pltpu.make_async_copy(outi, oi_hbm, out_sem.at[1])
        c_oi.start()
        wait_bytes(ear2.at[pl.ds(0, plane - 1)], ea2_r)
        eav = jnp.sum(ear2[...].astype(F32), axis=0)
        users_v = jnp.concatenate([eav[:, 0:DIM], pltpu.roll(eav, DIM, 1)[:, 0:DIM]], axis=0).astype(BF16)

        dots = lax.dot_general(oi[:, 0:DIM], users_v, (((1,), (1,)), ((), ())), preferred_element_type=F32)
        xp = jnp.sum(jnp.where(rowid == trips[1:2, :], dots, 0.0), axis=0, keepdims=True)
        xn = jnp.sum(jnp.where(rowid == trips[2:3, :], dots, 0.0), axis=0, keepdims=True)
        xs[me, 0:1, :] = xp - xn
        spread(xs.at[me, line], xs_s, xs_r)
        wait_bytes(xs.at[others, line], xs_r)
        xd[col, 0:1, :] = jnp.sum(xs[:, 0:1, :], axis=0)
        send(xd.at[col, line], xd.at[col, line], xd_s, xd_r, {"col": 1 - col})
        wait_bytes(xd.at[0, line], xd_r)
        neg = -(xd[0, 0:1, :] + xd[1, 0:1, :])
        sp = jnp.maximum(neg, 0.0) + jnp.log1p(jnp.exp(-jnp.abs(neg)))
        lossv[...] = jnp.sum(sp, axis=1, keepdims=True) * (1.0 / sp.shape[1])
        c_lo = pltpu.make_async_copy(lossv, loss_hbm, out_sem.at[2])
        c_lo.start()

        wait_bytes(deg.at[others], deg_s)
        wait_bytes(e0p.at[others], e0_s)
        wait_bytes(eu0t.at[0], eu0_s)
        wait_bytes(usum.at[0], us_s)
        for up, sem in ((up1, u1_s), (up2, u2_s), (up3, u3_s)):
            for k in range(2):
                wait_bytes(up.at[pl.ds(0, half // 2)], sem.at[k])
        wait_bytes(r1.at[others], r1_s)
        wait_bytes(r2.at[others], r2_s)
        wait_bytes(r3.at[others], r3_s)
        wait_bytes(g1.at[others], g1_s)
        wait_bytes(g2.at[others], g2_s)
        for o in range(1, side):
            wait_bytes(ea, ea1_s.at[o - 1])
        wait_bytes(ear2.at[pl.ds(0, plane - 1)], ea2_s)
        wait_bytes(xs.at[others, line], xs_s)
        wait_bytes(xd.at[0, line], xd_s)
        c_ou.wait()
        c_oi.wait()
        c_lo.wait()

    def local_prog(mask_blk, user_shard, item_shard, triples):
        users, items = mask_blk.shape
        half, dim = user_shard.shape
        shard = item_shard.shape[0]
        trips = triples.shape[0]
        V = pltpu.VMEM
        D = pltpu.SemaphoreType.DMA
        packed = (rows_n, shard // 2, LANES)
        scratch = [
            V((users, items), jnp.int32), V((users, items), BF16), V((items, users), BF16),
            V((8, items), F32), V((3, trips), jnp.int32),
            V((rows_n, items // LANES, LANES), F32), V((2, users // LANES, LANES), F32),
            V((users, LANES), F32), V((items // LANES, LANES), F32),
            V((2, dim, half), BF16), V((shard, dim), BF16), V(packed, BF16),
            V((users, LANES), BF16), V((items, LANES), BF16), V((items, LANES), BF16), V((items, LANES), BF16),
        ] + [V((half, LANES), F32)] * 6 + [V((users, LANES), BF16)] * 3 + [V(packed, F32)] * 6 + [V(packed, BF16)] * 2 + [
            V((users, LANES), BF16), V((dim, half), BF16), V((shard, dim), BF16),
            V((trips // 2, LANES), BF16), V((side - 1, trips // 2, LANES), BF16),
            V((trips // 2, LANES), BF16), V((plane, trips // 2, LANES), BF16),
            V((rows_n, 8, LANES), F32), V((2, 8, LANES), F32), V((1, 1), F32),
            D((users // LANES,)), D((3,)), D((3,)),
        ] + [D] * 8 + [D((2,))] * 6 + [D] * 10 + [D((side - 1,))] * 2 + [D] * 6
        ANY = pl.BlockSpec(memory_space=pl.ANY)
        out_user, out_item, loss = pl.pallas_call(
            kernel,
            out_shape=(jax.ShapeDtypeStruct((dim, half), BF16), jax.ShapeDtypeStruct((shard, dim), BF16),
                       jax.ShapeDtypeStruct((1, 1), F32)),
            in_specs=[ANY] * 4,
            out_specs=(ANY,) * 3,
            scratch_shapes=scratch,
            compiler_params=pltpu.CompilerParams(collective_id=0, has_side_effects=True,
                                                 vmem_limit_bytes=56 << 20),
        )(mask_blk, user_shard.T, item_shard, triples.T)
        return out_user.T, out_item, loss[0, 0]

    return jax.shard_map(local_prog, mesh=mesh, in_specs=(P("row", "col"), P(("row", "col"), None), P(("col", "row"), None), P(None, None)), out_specs=(P(("row", "col"), None), P(("col", "row"), None), P()), check_vma=False)
```

time: 98 us -> 75.5 us (0.77)
  Pallas kernels: 89.5 us -> 70.2 us
  local copies, waits for them, and re-layouts: 5.93 us -> 2.77 us
    pallas_call x1, Pallas kernels: 89.5 us -> 70.2 us  [local_prog(): pl.pallas_call(kernel, out_shape=(jax.ShapeDtypeStruct((dim, half), BF16)...]
    unnamed x4 -> x2, local copies, waits for them, and re-layouts: 5.93 us -> 2.77 us
where the time goes in v2:
time: 75.5 us; the launch traced here: 75.3 us
  Pallas kernels  70.2 us (93%)
  local copies, waits for them, and re-layouts  2.77 us (4%)
  between operations  2.33 us (3%)
    pallas_call x1, Pallas kernels, local_prog(): pl.pallas_call(kernel, out_shape=(jax.ShapeDtypeStruct((dim, half), BF16)...  70.2 us
    unnamed x2, local copies, waits for them, and re-layouts  2.77 us

profile of v2, /device:TPU:1, one launch (start us, length us, event | category | flops | bytes accessed | tf_op | source)
XLA Modules:
  0.0 75.3 jit_solution(1306400269964492874)
XLA Ops:
  0.6 70.2 %shard_map.67 = (bf16[64,512]{1,0:T(8,128)(2,1)}, bf16[32,64]{1,0:T(8,128)(2,1)}, f32[1,1]{1,0:T(1,128)}) custom-call(s32[1024,2048]{1,0:T(8,128)} %m_hbm.1, bf16[64,512]{1,0:T(8,128)(2,1)} %bitcast.4, bf16[32,64]{1,0:T(8,128)(2,1)} %ei_hbm.1, s32[3,128]{1,0:T(4,128)} %bitcast.6), custom_call_target="tpu_custom_call" | custom-call | tf_op jit(solution)/shard_map/pallas_call | solution.py:308
  70.8 1.5 %copy.10 = bf16[512,64]{0,1:T(8,128)(2,1)} copy(bf16[512,64]{0,1:T(8,128)(2,1)} %bitcast.5) | data formatting | bytes 131072
  72.3 1.3 %copy.11 = bf16[32,64]{1,0:T(8,128)(2,1)} copy(bf16[32,64]{1,0:T(8,128)(2,1)} %get-tuple-element.13) | data formatting | bytes 8192

commit v3 on v2

--- a/solution.py
+++ b/solution.py
@@ -23,13 +23,13 @@
     offsets = sorted(offsets[1:], key=lambda o: -(far(o[0]) + far(o[1]) + far(o[2])))
 
     def kernel(m_hbm, eu_hbm, ei_hbm, trip_hbm, ou_hbm, oi_hbm, loss_hbm,
-               m32, a, at, cacc, trip, deg, usum, suc, svr, eu0t, ei0, e0p, eu0d, e0d, pan1, pan2,
-               up1, ur1, up2, ur2, up3, ur3, eu1d, eu2d, eu3d, q1, q2, q3, r1, r2, r3, g1, g2, outd, outu, outi,
-               ea, ear1, ea1, ear2, xs, xd, lossv,
+               m32, a, at, cacc, trip, deg, usum, suc, svr, svc, eu0t, ei0, e0p, e0d, pan1, pan2,
+               up1, ur1, up2, ur2, up3, ur3, w0, w1, w2, eu0, eu1, eu2, eu3, q1, q2, q3, r1, r2, r3, g1, g2, outp, outu, outi,
+               ea, ear1, ea1, ear2, xs, lossv,
                m_sem, in_sem, out_sem,
                deg_s, deg_r, e0_s, e0_r, eu0_s, eu0_r, us_s, us_r, u1_s, u1_r, u2_s, u2_r, u3_s, u3_r,
                r1_s, r1_r, r2_s, r2_r, r3_s, r3_r, g1_s, g1_r, g2_s, g2_r,
-               ea1_s, ea1_r, ea2_s, ea2_r, xs_s, xs_r, xd_s, xd_r):
+               ea1_s, ea1_r, ea2_s, ea2_r, xs_s, xs_r):
         me = lax.axis_index("row")
         col = lax.axis_index("col")
         mx = me % side
@@ -78,6 +78,13 @@
                 return carry
             lax.fori_loop(0, rows_n // plane, body, 0)
 
+        def stack(v, w, k):
+            n = v.shape[0]
+            t = pltpu.roll(v, DIM, 1)
+            lo = lo_lanes(v)
+            for i, x in enumerate((jnp.where(lo, v, 0.0), jnp.where(lo, t, 0.0), jnp.where(lo, 0.0, t), jnp.where(lo, 0.0, v))):
+                w[i * half + k * n:i * half + (k + 1) * n, :] = x.astype(BF16)
+
         m_copies = []
         for b in range(ublk):
             blk = pl.ds(b * LANES, LANES)
@@ -92,6 +99,7 @@
         barrier = pltpu.get_barrier_semaphore()
         for o in offsets:
             pl.semaphore_signal(barrier, inc=1, device_id={"row": peer(o)})
+            pl.semaphore_signal(barrier, inc=1, device_id={"row": peer(o), "col": 1 - col})
         pl.semaphore_signal(barrier, inc=1, device_id={"col": 1 - col})
 
         cacc[...] = jnp.zeros_like(cacc)
@@ -113,7 +121,7 @@
         c_tr.wait()
         own0 = jnp.concatenate([ei0[...], ei0[...]], axis=1).astype(F32)
         e0p[me] = jnp.where(lo_lanes(own0[0:hs]), own0[0:hs], own0[hs:shard]).astype(BF16)
-        pl.semaphore_wait(barrier, rows_n)
+        pl.semaphore_wait(barrier, 2 * rows_n - 1)
         spread(deg.at[me], deg_s, deg_r)
         send(eu0t.at[col], eu0t.at[col], eu0_s, eu0_r, {"col": 1 - col})
 
@@ -126,7 +134,10 @@
 
         def flip(i, carry):
             c = pl.ds(pl.multiple_of(i * LANES, LANES), LANES)
-            at[c, :] = jnp.transpose(a[:, c])
+            t = jnp.transpose(a[:, c]).reshape(LANES // shard, 2, hs, users)
+            r = pl.ds(pl.multiple_of(i * LANES // 2, LANES // 2), LANES // 2)
+            at[r, 0:users] = t[:, 0].reshape(LANES // 2, users)
+            at[r, users:2 * users] = t[:, 1].reshape(LANES // 2, users)
             return carry
         lax.fori_loop(0, iblk, flip, 0)
         wait_bytes(usum.at[0], us_r)
@@ -134,30 +145,35 @@
         for b in range(ublk):
             suc[b * LANES:(b + 1) * LANES, :] = jnp.transpose(jnp.broadcast_to(su[b:b + 1, :], (LANES, LANES)))
         wait_bytes(eu0t.at[0], eu0_r)
-        for c in range(2):
-            t = eu0t[c]
-            eu0d[c * half:(c + 1) * half, :] = jnp.transpose(jnp.concatenate([t, t], axis=0))
+        eu0[...] = jnp.transpose(jnp.concatenate([eu0t[0], eu0t[1]], axis=0))
+        stack(eu0[...].astype(F32), w0, 0)
 
         wait_bytes(deg.at[others], deg_r)
-        svr[...] = lax.rsqrt(jnp.maximum(jnp.sum(deg[...], axis=0), 1.0))
+        sv = lax.rsqrt(jnp.maximum(jnp.sum(deg[...], axis=0), 1.0))
+        svr[...] = sv
+        svt = jnp.transpose(jnp.concatenate([sv, jnp.zeros((LANES - iblk, LANES), F32)], axis=0))
+        for i in range(iblk):
+            t = jnp.broadcast_to(svt[:, i:i + 1], (LANES, LANES)).reshape(LANES // shard, 2, hs, LANES)
+            for k in range(2):
+                svc[k, i * LANES // 2:(i + 1) * LANES // 2, :] = t[:, k].reshape(LANES // 2, LANES)
 
         def scale_at(i, carry):
             r = pl.ds(pl.multiple_of(i * LANES, LANES), LANES)
-            sv = jnp.transpose(jnp.broadcast_to(svr[pl.ds(i, 1), :], (LANES, LANES)))
-            for b in range(ublk):
-                c = slice(b * LANES, (b + 1) * LANES)
-                at[r, c] = at[r, c] * (su[b:b + 1, :] * sv).astype(BF16)
+            for k in range(2):
+                t = svc[k, r, :]
+                for b in range(ublk):
+                    c = slice(k * users + b * LANES, k * users + (b + 1) * LANES)
+                    at[r, c] = at[r, c] * (su[b:b + 1, :] * t).astype(BF16)
             return carry
-        lax.fori_loop(0, iblk, scale_at, 0)
-
-        def item_sums(eud, q, r, ssem, rsem):
-            step = plane * shard
+        lax.fori_loop(0, items // 2 // LANES, scale_at, 0)
+
+        def item_sums(w, q, r, ssem, rsem):
+            step = plane * hs
             for dz in sorted(range(side), key=lambda d: -far(d)):
                 z = pzs[dz]
-                rows = pl.ds(pl.multiple_of(z * shard, step), step)
-                v = jnp.dot(at[rows, :], eud[...], preferred_element_type=F32).reshape(plane, shard, LANES)
-                lo, hi = v[:, 0:hs, :], v[:, hs:shard, :]
-                q[pl.ds(z, plane)] = jnp.where(lo_lanes(lo), lo, hi)
+                rows = pl.ds(pl.multiple_of(z * hs, step), step)
+                v = jnp.dot(at[rows, :], w[...], preferred_element_type=F32)
+                q[pl.ds(z, plane)] = v.reshape(plane, hs, LANES)
                 for o in offsets:
                     if o[2] == dz:
                         p = peer(o)
@@ -172,26 +188,30 @@
                 up[k * h:(k + 1) * h, :] = jnp.where(lo_lanes(lo), lo, hi)
                 send(up.at[pl.ds(k * h, h)], ur.at[pl.ds(k * h, h)], ssem.at[k], rsem.at[k], {"col": 1 - col})
 
-        def user_rows(up, ur, rsem, eud):
+        def user_rows(up, ur, rsem, eu, w):
             h = half // 2
             for k in range(2):
                 wait_bytes(ur.at[pl.ds(k * h, h)], rsem.at[k])
                 s = up[k * h:(k + 1) * h, :] + ur[k * h:(k + 1) * h, :]
-                eud[k * h:(k + 1) * h, :] = dup_lo(s).astype(BF16)
-                eud[half + k * h:half + (k + 1) * h, :] = dup_hi(s).astype(BF16)
-
-        item_sums(eu0d, q1, r1, r1_s, r1_r)
-
-        def scale_a(i, carry):
-            c = pl.ds(pl.multiple_of(i * LANES, LANES), LANES)
-            a[:, c] = a[:, c] * (suc[...] * svr[pl.ds(i, 1), :]).astype(BF16)
+                eu[k * h:(k + 1) * h, :] = s.astype(BF16)
+                if w is not None:
+                    stack(s, w, k)
+
+        item_sums(w0, q1, r1, r1_s, r1_r)
+
+        def scale_a(b, carry):
+            r = pl.ds(pl.multiple_of(b * LANES, LANES), LANES)
+            t = suc[r, :]
+            for i in range(iblk):
+                c = slice(i * LANES, (i + 1) * LANES)
+                a[r, c] = a[r, c] * (t * svr[i:i + 1, :]).astype(BF16)
             return carry
-        lax.fori_loop(0, iblk, scale_a, 0)
+        lax.fori_loop(0, ublk, scale_a, 0)
         wait_bytes(e0p.at[others], e0_r)
         unpack(e0p, e0d)
         user_sums(e0d, up1, ur1, u1_s, u1_r)
-        user_rows(up1, ur1, u1_r, eu1d)
-        item_sums(eu1d, q2, r2, r2_s, r2_r)
+        user_rows(up1, ur1, u1_r, eu1, w1)
+        item_sums(w1, q2, r2, r2_s, r2_r)
         wait_bytes(r1.at[others], r1_r)
         g1[me] = jnp.sum(r1[...], axis=0).astype(BF16)
         spread(g1.at[me], g1_s, g1_r)
@@ -201,28 +221,29 @@
         wait_bytes(g1.at[others], g1_r)
         unpack(g1, pan1)
         user_sums(pan1, up2, ur2, u2_s, u2_r)
-        user_rows(up2, ur2, u2_r, eu2d)
-        item_sums(eu2d, q3, r3, r3_s, r3_r)
+        user_rows(up2, ur2, u2_r, eu2, w2)
+        item_sums(w2, q3, r3, r3_s, r3_r)
         wait_bytes(g2.at[others], g2_r)
         unpack(g2, pan2)
         user_sums(pan2, up3, ur3, u3_s, u3_r)
-        user_rows(up3, ur3, u3_r, eu3d)
-
-        quarter = users // 4
-        for k in range(4):
-            r = slice(k * quarter, (k + 1) * quarter)
-            t = eu0d[r, :].astype(F32) + eu1d[r, :].astype(F32) + eu2d[r, :].astype(F32) + eu3d[r, :].astype(F32)
-            outd[r, :] = (t * 0.25).astype(BF16)
+        user_rows(up3, ur3, u3_r, eu3, None)
+
+        t = eu0[...].astype(F32) + eu1[...].astype(F32) + eu2[...].astype(F32) + eu3[...].astype(F32)
+        outp[...] = (t * 0.25).astype(BF16)
         trips = trip[...]
         tn = trips.shape[1]
+        tq = tn // 2
         ids = lax.broadcasted_iota(jnp.int32, (users, tn), 0) + me * users
-        hot = jnp.where(ids == trips[0:1, :], 1.0, 0.0)
-        picked = jnp.dot(jnp.transpose(hot).astype(BF16), outd[...], preferred_element_type=F32)
-        tq = tn // 2
-        ea[...] = jnp.where(lo_lanes(picked[0:tq]), picked[0:tq], picked[tq:tn]).astype(BF16)
+        hot = jnp.transpose(jnp.where(ids == trips[0:1, :], 1.0, 0.0)).astype(BF16)
+        first = jnp.dot(hot[:, 0:half], outp[...], preferred_element_type=F32)
+        second = jnp.dot(hot[:, half:users], outp[...], preferred_element_type=F32)
+        top = first[0:tq] + pltpu.roll(second[0:tq], DIM, 1)
+        bot = pltpu.roll(first[tq:tn], DIM, 1) + second[tq:tn]
+        ea[...] = jnp.where(lo_lanes(top), top, bot).astype(BF16)
         for o in (2, 1, 3):
             send(ea, ear1.at[o - 1], ea1_s.at[o - 1], ea1_r.at[o - 1], {"row": pxs[o] + pys[0] + pzs[0]})
-        outu[...] = jnp.transpose(outd[pl.ds(pl.multiple_of(col * half, half), half), :])[0:DIM, :]
+        flat = jnp.transpose(outp[...])
+        outu[...] = jnp.where(col == 0, flat[0:DIM, :], flat[DIM:2 * DIM, :])
         c_ou = pltpu.make_async_copy(outu, ou_hbm, out_sem.at[0])
         c_ou.start()
         for o in range(1, side):
@@ -249,13 +270,14 @@
         dots = lax.dot_general(oi[:, 0:DIM], users_v, (((1,), (1,)), ((), ())), preferred_element_type=F32)
         xp = jnp.sum(jnp.where(rowid == trips[1:2, :], dots, 0.0), axis=0, keepdims=True)
         xn = jnp.sum(jnp.where(rowid == trips[2:3, :], dots, 0.0), axis=0, keepdims=True)
-        xs[me, 0:1, :] = xp - xn
-        spread(xs.at[me, line], xs_s, xs_r)
-        wait_bytes(xs.at[others, line], xs_r)
-        xd[col, 0:1, :] = jnp.sum(xs[:, 0:1, :], axis=0)
-        send(xd.at[col, line], xd.at[col, line], xd_s, xd_r, {"col": 1 - col})
-        wait_bytes(xd.at[0, line], xd_r)
-        neg = -(xd[0, 0:1, :] + xd[1, 0:1, :])
+        mine = col * rows_n + me
+        xs[mine, 0:1, :] = xp - xn
+        for o in offsets:
+            for c in (1 - col, col):
+                send(xs.at[mine, line], xs.at[mine, line], xs_s, xs_r, {"row": peer(o), "col": c})
+        send(xs.at[mine, line], xs.at[mine, line], xs_s, xs_r, {"col": 1 - col})
+        wait_bytes(xs.at[pl.ds(0, 2 * rows_n - 1), line], xs_r)
+        neg = -jnp.sum(xs[:, 0:1, :], axis=0)
         sp = jnp.maximum(neg, 0.0) + jnp.log1p(jnp.exp(-jnp.abs(neg)))
         lossv[...] = jnp.sum(sp, axis=1, keepdims=True) * (1.0 / sp.shape[1])
         c_lo = pltpu.make_async_copy(lossv, loss_hbm, out_sem.at[2])
@@ -276,8 +298,7 @@
         for o in range(1, side):
             wait_bytes(ea, ea1_s.at[o - 1])
         wait_bytes(ear2.at[pl.ds(0, plane - 1)], ea2_s)
-        wait_bytes(xs.at[others, line], xs_s)
-        wait_bytes(xd.at[0, line], xd_s)
+        wait_bytes(xs.at[pl.ds(0, 2 * rows_n - 1), line], xs_s)
         c_ou.wait()
         c_oi.wait()
         c_lo.wait()
@@ -291,19 +312,19 @@
         D = pltpu.SemaphoreType.DMA
         packed = (rows_n, shard // 2, LANES)
         scratch = [
-            V((users, items), jnp.int32), V((users, items), BF16), V((items, users), BF16),
+            V((users, items), jnp.int32), V((users, items), BF16), V((items // 2, 2 * users), BF16),
             V((8, items), F32), V((3, trips), jnp.int32),
             V((rows_n, items // LANES, LANES), F32), V((2, users // LANES, LANES), F32),
-            V((users, LANES), F32), V((items // LANES, LANES), F32),
+            V((users, LANES), F32), V((items // LANES, LANES), F32), V((2, items // 2, LANES), F32),
             V((2, dim, half), BF16), V((shard, dim), BF16), V(packed, BF16),
-            V((users, LANES), BF16), V((items, LANES), BF16), V((items, LANES), BF16), V((items, LANES), BF16),
-        ] + [V((half, LANES), F32)] * 6 + [V((users, LANES), BF16)] * 3 + [V(packed, F32)] * 6 + [V(packed, BF16)] * 2 + [
-            V((users, LANES), BF16), V((dim, half), BF16), V((shard, dim), BF16),
+        ] + [V((items, LANES), BF16)] * 3 + [V((half, LANES), F32)] * 6 + [V((2 * users, LANES), BF16)] * 3 + [
+            V((half, LANES), BF16)] * 4 + [V(packed, F32)] * 6 + [V(packed, BF16)] * 2 + [
+            V((half, LANES), BF16), V((dim, half), BF16), V((shard, dim), BF16),
             V((trips // 2, LANES), BF16), V((side - 1, trips // 2, LANES), BF16),
             V((trips // 2, LANES), BF16), V((plane, trips // 2, LANES), BF16),
-            V((rows_n, 8, LANES), F32), V((2, 8, LANES), F32), V((1, 1), F32),
+            V((2 * rows_n, 8, LANES), F32), V((1, 1), F32),
             D((users // LANES,)), D((3,)), D((3,)),
-        ] + [D] * 8 + [D((2,))] * 6 + [D] * 10 + [D((side - 1,))] * 2 + [D] * 6
+        ] + [D] * 8 + [D((2,))] * 6 + [D] * 10 + [D((side - 1,))] * 2 + [D] * 4
         ANY = pl.BlockSpec(memory_space=pl.ANY)
         out_user, out_item, loss = pl.pallas_call(
             kernel,

time: 75.5 us -> 71.9 us (0.952)
  Pallas kernels: 70.2 us -> 66.6 us
    pallas_call x1, Pallas kernels: 70.2 us -> 66.6 us  [local_prog(): pl.pallas_call(kernel, out_shape=(jax.ShapeDtypeStruct((dim, half), BF16)...]
where the time goes in v3:
time: 71.9 us; the launch traced here: 71.7 us
  Pallas kernels  66.6 us (93%)
  local copies, waits for them, and re-layouts  2.77 us (4%)
  between operations  2.33 us (3%)
    pallas_call x1, Pallas kernels, local_prog(): pl.pallas_call(kernel, out_shape=(jax.ShapeDtypeStruct((dim, half), BF16)...  66.6 us
    unnamed x2, local copies, waits for them, and re-layouts  2.77 us

profile of v3, /device:TPU:1, one launch (start us, length us, event | category | flops | bytes accessed | tf_op | source)
XLA Modules:
  0.0 71.7 jit_solution(6898335313302553306)
XLA Ops:
  0.6 66.6 %shard_map.67 = (bf16[64,512]{1,0:T(8,128)(2,1)}, bf16[32,64]{1,0:T(8,128)(2,1)}, f32[1,1]{1,0:T(1,128)}) custom-call(s32[1024,2048]{1,0:T(8,128)} %m_hbm.1, bf16[64,512]{1,0:T(8,128)(2,1)} %bitcast.4, bf16[32,64]{1,0:T(8,128)(2,1)} %ei_hbm.1, s32[3,128]{1,0:T(4,128)} %bitcast.6), custom_call_target="tpu_custom_call" | custom-call | tf_op jit(solution)/shard_map/pallas_call | solution.py:329
  67.2 1.5 %copy.10 = bf16[512,64]{0,1:T(8,128)(2,1)} copy(bf16[512,64]{0,1:T(8,128)(2,1)} %bitcast.5) | data formatting | bytes 131072
  68.7 1.3 %copy.11 = bf16[32,64]{1,0:T(8,128)(2,1)} copy(bf16[32,64]{1,0:T(8,128)(2,1)} %get-tuple-element.13) | data formatting | bytes 8192

commit v4 on v3

--- a/solution.py
+++ b/solution.py
@@ -25,7 +25,7 @@
     def kernel(m_hbm, eu_hbm, ei_hbm, trip_hbm, ou_hbm, oi_hbm, loss_hbm,
                m32, a, at, cacc, trip, deg, usum, suc, svr, svc, eu0t, ei0, e0p, e0d, pan1, pan2,
                up1, ur1, up2, ur2, up3, ur3, w0, w1, w2, eu0, eu1, eu2, eu3, q1, q2, q3, r1, r2, r3, g1, g2, outp, outu, outi,
-               ea, ear1, ea1, ear2, xs, lossv,
+               ea, ear1, ea1, ear2, xs, lossv, hot,
                m_sem, in_sem, out_sem,
                deg_s, deg_r, e0_s, e0_r, eu0_s, eu0_r, us_s, us_r, u1_s, u1_r, u2_s, u2_r, u3_s, u3_r,
                r1_s, r1_r, r2_s, r2_r, r3_s, r3_r, g1_s, g1_r, g2_s, g2_r,
@@ -38,6 +38,8 @@
         pxs = [(mx + d) % side for d in range(side)]
         pys = [((my + d) % side) * side for d in range(side)]
         pzs = [((mz + d) % side) * plane for d in range(side)]
+        nxs = [(d - mx + side) % side for d in range(side)]
+        nys = [((d - my + side) % side) * side for d in range(side)]
         users, items = a.shape
         half = users // 2
         shard = items // rows_n
@@ -130,16 +132,22 @@
             rsum = jnp.dot(a[b * LANES:(b + 1) * LANES, :], ones, preferred_element_type=F32)
             usum[col, b:b + 1, :] = jnp.transpose(rsum)[0:1, :]
         send(usum.at[col], usum.at[col], us_s, us_r, {"col": 1 - col})
-        spread(e0p.at[me], e0_s, e0_r)
-
         def flip(i, carry):
             c = pl.ds(pl.multiple_of(i * LANES, LANES), LANES)
-            t = jnp.transpose(a[:, c]).reshape(LANES // shard, 2, hs, users)
-            r = pl.ds(pl.multiple_of(i * LANES // 2, LANES // 2), LANES // 2)
-            at[r, 0:users] = t[:, 0].reshape(LANES // 2, users)
-            at[r, users:2 * users] = t[:, 1].reshape(LANES // 2, users)
+            t = jnp.transpose(a[:, c])
+            n = ((i % side - my + side) % side) * side + ((i // side - mz + side) % side) * plane
+            for x in range(side):
+                r = pl.ds(pl.multiple_of((n + nxs[x]) * hs, hs), hs)
+                at[r, 0:users] = t[x * shard:x * shard + hs]
+                at[r, users:2 * users] = t[x * shard + hs:(x + 1) * shard]
             return carry
         lax.fori_loop(0, iblk, flip, 0)
+        spread(e0p.at[me], e0_s, e0_r)
+        trips = trip[...]
+        tn = trips.shape[1]
+        tq = tn // 2
+        ids = lax.broadcasted_iota(jnp.int32, (users, tn), 0) + me * users
+        hot[...] = jnp.transpose(jnp.where(ids == trips[0:1, :], 1.0, 0.0)).astype(BF16)
         wait_bytes(usum.at[0], us_r)
         su = lax.rsqrt(jnp.maximum(usum[0] + usum[1], 1.0))
         for b in range(ublk):
@@ -153,9 +161,12 @@
         svr[...] = sv
         svt = jnp.transpose(jnp.concatenate([sv, jnp.zeros((LANES - iblk, LANES), F32)], axis=0))
         for i in range(iblk):
-            t = jnp.broadcast_to(svt[:, i:i + 1], (LANES, LANES)).reshape(LANES // shard, 2, hs, LANES)
-            for k in range(2):
-                svc[k, i * LANES // 2:(i + 1) * LANES // 2, :] = t[:, k].reshape(LANES // 2, LANES)
+            t = jnp.broadcast_to(svt[:, i:i + 1], (LANES, LANES))
+            n = nys[i % side] + ((i // side - mz + side) % side) * plane
+            for x in range(side):
+                r = pl.ds(pl.multiple_of((n + nxs[x]) * hs, hs), hs)
+                svc[0, r, :] = t[x * shard:x * shard + hs]
+                svc[1, r, :] = t[x * shard + hs:(x + 1) * shard]
 
         def scale_at(i, carry):
             r = pl.ds(pl.multiple_of(i * LANES, LANES), LANES)
@@ -168,24 +179,21 @@
         lax.fori_loop(0, items // 2 // LANES, scale_at, 0)
 
         def item_sums(w, q, r, ssem, rsem):
-            step = plane * hs
             for dz in sorted(range(side), key=lambda d: -far(d)):
-                z = pzs[dz]
-                rows = pl.ds(pl.multiple_of(z * hs, step), step)
-                v = jnp.dot(at[rows, :], w[...], preferred_element_type=F32)
-                q[pl.ds(z, plane)] = v.reshape(plane, hs, LANES)
+                v = jnp.dot(at[dz * plane * hs:(dz + 1) * plane * hs, :], w[...], preferred_element_type=F32)
+                q[dz * plane:(dz + 1) * plane] = v.reshape(plane, hs, LANES)
                 for o in offsets:
                     if o[2] == dz:
-                        p = peer(o)
-                        send(q.at[p], r.at[me], ssem, rsem, {"row": p})
-            r[me] = q[me]
+                        send(q.at[o[0] + side * o[1] + plane * o[2]], r.at[me], ssem, rsem, {"row": peer(o)})
+            r[me] = q[0]
 
         def user_sums(pan, up, ur, ssem, rsem):
             h = half // 2
             for k in range(2):
+                r = slice(k * h, (k + 1) * h)
                 lo = jnp.dot(a[k * h:(k + 1) * h, :], pan[...], preferred_element_type=F32)
                 hi = jnp.dot(a[half + k * h:half + (k + 1) * h, :], pan[...], preferred_element_type=F32)
-                up[k * h:(k + 1) * h, :] = jnp.where(lo_lanes(lo), lo, hi)
+                up[r, :] = jnp.where(lo_lanes(lo), lo, hi)
                 send(up.at[pl.ds(k * h, h)], ur.at[pl.ds(k * h, h)], ssem.at[k], rsem.at[k], {"col": 1 - col})
 
         def user_rows(up, ur, rsem, eu, w):
@@ -230,28 +238,21 @@
 
         t = eu0[...].astype(F32) + eu1[...].astype(F32) + eu2[...].astype(F32) + eu3[...].astype(F32)
         outp[...] = (t * 0.25).astype(BF16)
-        trips = trip[...]
-        tn = trips.shape[1]
-        tq = tn // 2
-        ids = lax.broadcasted_iota(jnp.int32, (users, tn), 0) + me * users
-        hot = jnp.transpose(jnp.where(ids == trips[0:1, :], 1.0, 0.0)).astype(BF16)
         first = jnp.dot(hot[:, 0:half], outp[...], preferred_element_type=F32)
         second = jnp.dot(hot[:, half:users], outp[...], preferred_element_type=F32)
         top = first[0:tq] + pltpu.roll(second[0:tq], DIM, 1)
         bot = pltpu.roll(first[tq:tn], DIM, 1) + second[tq:tn]
         ea[...] = jnp.where(lo_lanes(top), top, bot).astype(BF16)
         for o in (2, 1, 3):
-            send(ea, ear1.at[o - 1], ea1_s.at[o - 1], ea1_r.at[o - 1], {"row": pxs[o] + pys[0] + pzs[0]})
+            send(ea, ear1.at[o - 1], ea1_s.at[o - 1], ea1_r.at[o - 1], {"row": pxs[0] + pys[0] + pzs[o]})
         flat = jnp.transpose(outp[...])
-        outu[...] = jnp.where(col == 0, flat[0:DIM, :], flat[DIM:2 * DIM, :])
-        c_ou = pltpu.make_async_copy(outu, ou_hbm, out_sem.at[0])
-        c_ou.start()
+        ou_hbm[...] = jnp.where(col == 0, flat[0:DIM, :], flat[DIM:2 * DIM, :])
         for o in range(1, side):
             wait_bytes(ear1.at[o - 1], ea1_r.at[o - 1])
         ea1[...] = (ea[...].astype(F32) + jnp.sum(ear1[...].astype(F32), axis=0)).astype(BF16)
         for o in offsets:
-            if o[0] == 0:
-                send(ea1, ear2.at[o[1] + side * o[2]], ea2_s, ea2_r, {"row": peer(o)})
+            if o[2] == 0:
+                send(ea1, ear2.at[o[0] + side * o[1]], ea2_s, ea2_r, {"row": peer(o)})
         ear2[0] = ea1[...]
         g = g1[me].astype(F32)
         h = g2[me].astype(F32)
@@ -260,9 +261,7 @@
         wait_bytes(r3.at[others], r3_r)
         s3 = jnp.sum(r3[...], axis=0).astype(BF16).astype(F32)
         oi = ((tot + jnp.concatenate([dup_lo(s3), dup_hi(s3)], axis=0)) * 0.25).astype(BF16)
-        outi[...] = oi[:, 0:DIM]
-        c_oi = pltpu.make_async_copy(outi, oi_hbm, out_sem.at[1])
-        c_oi.start()
+        oi_hbm[...] = oi[:, 0:DIM]
         wait_bytes(ear2.at[pl.ds(0, plane - 1)], ea2_r)
         eav = jnp.sum(ear2[...].astype(F32), axis=0)
         users_v = jnp.concatenate([eav[:, 0:DIM], pltpu.roll(eav, DIM, 1)[:, 0:DIM]], axis=0).astype(BF16)
@@ -279,9 +278,7 @@
         wait_bytes(xs.at[pl.ds(0, 2 * rows_n - 1), line], xs_r)
         neg = -jnp.sum(xs[:, 0:1, :], axis=0)
         sp = jnp.maximum(neg, 0.0) + jnp.log1p(jnp.exp(-jnp.abs(neg)))
-        lossv[...] = jnp.sum(sp, axis=1, keepdims=True) * (1.0 / sp.shape[1])
-        c_lo = pltpu.make_async_copy(lossv, loss_hbm, out_sem.at[2])
-        c_lo.start()
+        loss_hbm[...] = jnp.sum(sp, axis=1, keepdims=True) * (1.0 / sp.shape[1])
 
         wait_bytes(deg.at[others], deg_s)
         wait_bytes(e0p.at[others], e0_s)
@@ -299,9 +296,6 @@
             wait_bytes(ea, ea1_s.at[o - 1])
         wait_bytes(ear2.at[pl.ds(0, plane - 1)], ea2_s)
         wait_bytes(xs.at[pl.ds(0, 2 * rows_n - 1), line], xs_s)
-        c_ou.wait()
-        c_oi.wait()
-        c_lo.wait()
 
     def local_prog(mask_blk, user_shard, item_shard, triples):
         users, items = mask_blk.shape
@@ -322,16 +316,15 @@
             V((half, LANES), BF16), V((dim, half), BF16), V((shard, dim), BF16),
             V((trips // 2, LANES), BF16), V((side - 1, trips // 2, LANES), BF16),
             V((trips // 2, LANES), BF16), V((plane, trips // 2, LANES), BF16),
-            V((2 * rows_n, 8, LANES), F32), V((1, 1), F32),
+            V((2 * rows_n, 8, LANES), F32), V((1, 1), F32), V((trips, users), BF16),
             D((users // LANES,)), D((3,)), D((3,)),
         ] + [D] * 8 + [D((2,))] * 6 + [D] * 10 + [D((side - 1,))] * 2 + [D] * 4
         ANY = pl.BlockSpec(memory_space=pl.ANY)
         out_user, out_item, loss = pl.pallas_call(
             kernel,
-            out_shape=(jax.ShapeDtypeStruct((dim, half), BF16), jax.ShapeDtypeStruct((shard, dim), BF16),
-                       jax.ShapeDtypeStruct((1, 1), F32)),
+            out_shape=(pltpu.VMEM((dim, half), BF16), pltpu.VMEM((shard, dim), BF16), pltpu.VMEM((1, 1), F32)),
             in_specs=[ANY] * 4,
-            out_specs=(ANY,) * 3,
+            out_specs=(pl.BlockSpec(memory_space=pltpu.VMEM),) * 3,
             scratch_shapes=scratch,
             compiler_params=pltpu.CompilerParams(collective_id=0, has_side_effects=True,
                                                  vmem_limit_bytes=56 << 20),

time: 71.9 us -> 69.3 us (0.964)
  local copies, waits for them, and re-layouts: 2.77 us -> 1.23 us
    unnamed x2, local copies, waits for them, and re-layouts: 2.77 us -> 1.23 us
where the time goes in v4:
time: 69.3 us; the launch traced here: 69.2 us
  Pallas kernels  66.1 us (95%)
  between operations  1.8 us (3%)
  local copies, waits for them, and re-layouts  1.23 us (2%)
    pallas_call x1, Pallas kernels, local_prog(): pl.pallas_call(kernel, out_shape=(pltpu.VMEM((dim, half), BF16), pltpu.VM...  66.1 us

profile of v4, /device:TPU:1, one launch (start us, length us, event | category | flops | bytes accessed | tf_op | source)
XLA Modules:
  0.0 69.2 jit_solution(9110040330178952949)
XLA Ops:
  0.6 66.1 %shard_map.67 = (bf16[64,512]{1,0:T(8,128)(2,1)S(1)}, bf16[32,64]{1,0:T(8,128)(2,1)S(1)}, f32[1,1]{1,0:T(1,128)S(1)}) custom-call(s32[1024,2048]{1,0:T(8,128)} %m_hbm.1, bf16[64,512]{1,0:T(8,128)(2,1)} %bitcast.5, bf16[32,64]{1,0:T(8,128)(2,1)} %ei_hbm.1, s32[3,128]{1,0:T(4,128)} %bitcast.6), custom_call_target="tpu_custom_call" | custom-call | tf_op jit(solution)/shard_map/pallas_call | solution.py:323
  66.8 0.6 copy.10
  67.4 0.6 copy.11

commit v5 on v4

--- a/solution.py
+++ b/solution.py
@@ -24,12 +24,12 @@
 
     def kernel(m_hbm, eu_hbm, ei_hbm, trip_hbm, ou_hbm, oi_hbm, loss_hbm,
                m32, a, at, cacc, trip, deg, usum, suc, svr, svc, eu0t, ei0, e0p, e0d, pan1, pan2,
-               up1, ur1, up2, ur2, up3, ur3, w0, w1, w2, eu0, eu1, eu2, eu3, q1, q2, q3, r1, r2, r3, g1, g2, outp, outu, outi,
-               ea, ear1, ea1, ear2, xs, lossv, hot,
+               up1, ur1, up2, ur2, up3, ur3, w0, w1, w2, eu0, eu1, eu2, eu3, q1, q2, q3, r1, r2, t3, m3, f3, g1, g2, outp, outu, outi,
+               ea, ear1, ea1, ear2, ea3, xs, lossv, hot,
                m_sem, in_sem, out_sem,
                deg_s, deg_r, e0_s, e0_r, eu0_s, eu0_r, us_s, us_r, u1_s, u1_r, u2_s, u2_r, u3_s, u3_r,
                r1_s, r1_r, r2_s, r2_r, r3_s, r3_r, g1_s, g1_r, g2_s, g2_r,
-               ea1_s, ea1_r, ea2_s, ea2_r, xs_s, xs_r):
+               ea1_s, ea1_r, ea2_s, ea2_r, xs_s, xs_r, f3_s, f3_r, ea3_s, ea3_r):
         me = lax.axis_index("row")
         col = lax.axis_index("col")
         mx = me % side
@@ -47,6 +47,7 @@
         ublk = users // LANES
         iblk = items // LANES
         others = pl.ds(0, rows_n - 1)
+        axes3 = (0, 1)
         line = pl.ds(0, 1)
 
         def peer(o):
@@ -187,6 +188,46 @@
                         send(q.at[o[0] + side * o[1] + plane * o[2]], r.at[me], ssem, rsem, {"row": peer(o)})
             r[me] = q[0]
 
+        def axis_view(ref, axis, d, part):
+            return (ref.at[:, :, d, part], ref.at[:, d, :, part], ref.at[d, :, :, part])[axis]
+
+        def axis_peer(axis, d):
+            o = [0, 0, 0]
+            o[axis] = d
+            return peer(o)
+
+        def item_dots(w, q):
+            for dz in range(side):
+                v = jnp.dot(at[dz * plane * hs:(dz + 1) * plane * hs, :], w[...], preferred_element_type=F32)
+                q[dz] = v.reshape(side, side, hs, LANES)
+
+        def lines_start(q, axes, tmp, ssem, rsem):
+            n = hs // len(axes)
+            for k, axis in enumerate(axes):
+                for d in sorted(range(1, side), key=lambda d: -far(d)):
+                    send(axis_view(q, axis, d, pl.ds(k * n, n)), tmp.at[k, d - 1], ssem.at[k, d - 1], rsem.at[k, d - 1],
+                         {"row": axis_peer(axis, d)})
+
+        def planes_start(q, axes, tmp, mid, fin, rsem, ssem2, rsem2):
+            n = hs // len(axes)
+            for k, axis in enumerate(axes):
+                for d in range(1, side):
+                    wait_bytes(tmp.at[k, d - 1], rsem.at[k, d - 1])
+                own = axis_view(q, axis, 0, pl.ds(k * n, n))[...]
+                mid[k] = own + tmp[k, 0] + tmp[k, 1] + tmp[k, 2]
+                for o in offsets:
+                    if o[axis] == 0:
+                        u, v = [o[i] for i in range(3) if i != axis]
+                        send(mid.at[k, v, u], fin.at[k, v * side + u], ssem2.at[k], rsem2.at[k], {"row": peer(o)})
+                fin[k, 0] = mid[k, 0, 0]
+
+        def planes_done(axes, fin, rsem2):
+            out = []
+            for k in range(len(axes)):
+                wait_bytes(fin.at[k, pl.ds(0, plane - 1)], rsem2.at[k])
+                out.append(jnp.sum(fin[k], axis=0))
+            return jnp.concatenate(out, axis=0)
+
         def user_sums(pan, up, ur, ssem, rsem):
             h = half // 2
             for k in range(2):
@@ -230,7 +271,8 @@
         unpack(g1, pan1)
         user_sums(pan1, up2, ur2, u2_s, u2_r)
         user_rows(up2, ur2, u2_r, eu2, w2)
-        item_sums(w2, q3, r3, r3_s, r3_r)
+        item_dots(w2, q3)
+        lines_start(q3, axes3, t3, r3_s, r3_r)
         wait_bytes(g2.at[others], g2_r)
         unpack(g2, pan2)
         user_sums(pan2, up3, ur3, u3_s, u3_r)
@@ -240,11 +282,14 @@
         outp[...] = (t * 0.25).astype(BF16)
         first = jnp.dot(hot[:, 0:half], outp[...], preferred_element_type=F32)
         second = jnp.dot(hot[:, half:users], outp[...], preferred_element_type=F32)
-        top = first[0:tq] + pltpu.roll(second[0:tq], DIM, 1)
-        bot = pltpu.roll(first[tq:tn], DIM, 1) + second[tq:tn]
+        mine = jnp.where(col == 0, first[0:tq], first[tq:tn])
+        rest = jnp.where(col == 0, second[0:tq], second[tq:tn])
+        top = mine[0:tq // 2] + pltpu.roll(rest[0:tq // 2], DIM, 1)
+        bot = pltpu.roll(mine[tq // 2:tq], DIM, 1) + rest[tq // 2:tq]
         ea[...] = jnp.where(lo_lanes(top), top, bot).astype(BF16)
         for o in (2, 1, 3):
             send(ea, ear1.at[o - 1], ea1_s.at[o - 1], ea1_r.at[o - 1], {"row": pxs[0] + pys[0] + pzs[o]})
+        planes_start(q3, axes3, t3, m3, f3, r3_r, f3_s, f3_r)
         flat = jnp.transpose(outp[...])
         ou_hbm[...] = jnp.where(col == 0, flat[0:DIM, :], flat[DIM:2 * DIM, :])
         for o in range(1, side):
@@ -258,23 +303,28 @@
         h = g2[me].astype(F32)
         tot = (own0 + jnp.concatenate([dup_lo(g), dup_hi(g)], axis=0)) + jnp.concatenate([dup_lo(h), dup_hi(h)], axis=0)
         rowid = lax.broadcasted_iota(jnp.int32, (shard, LANES), 0) + (col * items + me * shard)
-        wait_bytes(r3.at[others], r3_r)
-        s3 = jnp.sum(r3[...], axis=0).astype(BF16).astype(F32)
+        s3 = planes_done(axes3, f3, f3_r).astype(BF16).astype(F32)
         oi = ((tot + jnp.concatenate([dup_lo(s3), dup_hi(s3)], axis=0)) * 0.25).astype(BF16)
         oi_hbm[...] = oi[:, 0:DIM]
         wait_bytes(ear2.at[pl.ds(0, plane - 1)], ea2_r)
-        eav = jnp.sum(ear2[...].astype(F32), axis=0)
-        users_v = jnp.concatenate([eav[:, 0:DIM], pltpu.roll(eav, DIM, 1)[:, 0:DIM]], axis=0).astype(BF16)
+        ea3[col] = jnp.sum(ear2[...].astype(F32), axis=0).astype(BF16)
+        send(ea3.at[col], ea3.at[col], ea3_s, ea3_r, {"col": 1 - col})
+        wait_bytes(ea3.at[0], ea3_r)
+        halves = []
+        for c in range(2):
+            v = ea3[c].astype(F32)
+            halves += [v[:, 0:DIM], pltpu.roll(v, DIM, 1)[:, 0:DIM]]
+        users_v = jnp.concatenate(halves, axis=0).astype(BF16)
 
         dots = lax.dot_general(oi[:, 0:DIM], users_v, (((1,), (1,)), ((), ())), preferred_element_type=F32)
         xp = jnp.sum(jnp.where(rowid == trips[1:2, :], dots, 0.0), axis=0, keepdims=True)
         xn = jnp.sum(jnp.where(rowid == trips[2:3, :], dots, 0.0), axis=0, keepdims=True)
-        mine = col * rows_n + me
-        xs[mine, 0:1, :] = xp - xn
+        slot = col * rows_n + me
+        xs[slot, 0:1, :] = xp - xn
         for o in offsets:
             for c in (1 - col, col):
-                send(xs.at[mine, line], xs.at[mine, line], xs_s, xs_r, {"row": peer(o), "col": c})
-        send(xs.at[mine, line], xs.at[mine, line], xs_s, xs_r, {"col": 1 - col})
+                send(xs.at[slot, line], xs.at[slot, line], xs_s, xs_r, {"row": peer(o), "col": c})
+        send(xs.at[slot, line], xs.at[slot, line], xs_s, xs_r, {"col": 1 - col})
         wait_bytes(xs.at[pl.ds(0, 2 * rows_n - 1), line], xs_r)
         neg = -jnp.sum(xs[:, 0:1, :], axis=0)
         sp = jnp.maximum(neg, 0.0) + jnp.log1p(jnp.exp(-jnp.abs(neg)))
@@ -289,12 +339,16 @@
                 wait_bytes(up.at[pl.ds(0, half // 2)], sem.at[k])
         wait_bytes(r1.at[others], r1_s)
         wait_bytes(r2.at[others], r2_s)
-        wait_bytes(r3.at[others], r3_s)
+        for k in range(2):
+            for d in range(side - 1):
+                wait_bytes(t3.at[k, d], r3_s.at[k, d])
+            wait_bytes(f3.at[k, pl.ds(0, plane - 1)], f3_s.at[k])
         wait_bytes(g1.at[others], g1_s)
         wait_bytes(g2.at[others], g2_s)
         for o in range(1, side):
             wait_bytes(ea, ea1_s.at[o - 1])
         wait_bytes(ear2.at[pl.ds(0, plane - 1)], ea2_s)
+        wait_bytes(ea3.at[0], ea3_s)
         wait_bytes(xs.at[pl.ds(0, 2 * rows_n - 1), line], xs_s)
 
     def local_prog(mask_blk, user_shard, item_shard, triples):
@@ -305,6 +359,8 @@
         V = pltpu.VMEM
         D = pltpu.SemaphoreType.DMA
         packed = (rows_n, shard // 2, LANES)
+        cube = (side, side, side, shard // 2, LANES)
+        step = (side, side, shard // 4, LANES)
         scratch = [
             V((users, items), jnp.int32), V((users, items), BF16), V((items // 2, 2 * users), BF16),
             V((8, items), F32), V((3, trips), jnp.int32),
@@ -312,13 +368,14 @@
             V((users, LANES), F32), V((items // LANES, LANES), F32), V((2, items // 2, LANES), F32),
             V((2, dim, half), BF16), V((shard, dim), BF16), V(packed, BF16),
         ] + [V((items, LANES), BF16)] * 3 + [V((half, LANES), F32)] * 6 + [V((2 * users, LANES), BF16)] * 3 + [
-            V((half, LANES), BF16)] * 4 + [V(packed, F32)] * 6 + [V(packed, BF16)] * 2 + [
+            V((half, LANES), BF16)] * 4 + [V(packed, F32)] * 2 + [V(cube, F32)] + [V(packed, F32)] * 2 + [
+            V((2, side - 1) + step, F32), V((2,) + step, F32), V((2, plane) + step[2:], F32)] + [V(packed, BF16)] * 2 + [
             V((half, LANES), BF16), V((dim, half), BF16), V((shard, dim), BF16),
-            V((trips // 2, LANES), BF16), V((side - 1, trips // 2, LANES), BF16),
-            V((trips // 2, LANES), BF16), V((plane, trips // 2, LANES), BF16),
+            V((trips // 4, LANES), BF16), V((side - 1, trips // 4, LANES), BF16),
+            V((trips // 4, LANES), BF16), V((plane, trips // 4, LANES), BF16), V((2, trips // 4, LANES), BF16),
             V((2 * rows_n, 8, LANES), F32), V((1, 1), F32), V((trips, users), BF16),
             D((users // LANES,)), D((3,)), D((3,)),
-        ] + [D] * 8 + [D((2,))] * 6 + [D] * 10 + [D((side - 1,))] * 2 + [D] * 4
+        ] + [D] * 8 + [D((2,))] * 6 + [D] * 4 + [D((2, side - 1))] * 2 + [D] * 4 + [D((side - 1,))] * 2 + [D] * 4 + [D((2,))] * 2 + [D] * 2
         ANY = pl.BlockSpec(memory_space=pl.ANY)
         out_user, out_item, loss = pl.pallas_call(
             kernel,

time: 69.3 us -> 67.6 us (0.975)
  Pallas kernels: 66.1 us -> 64.5 us
    pallas_call x1, Pallas kernels: 66.1 us -> 64.5 us  [local_prog(): pl.pallas_call(kernel, out_shape=(pltpu.VMEM((dim, half), BF16), pltpu.VM...]
where the time goes in v5:
time: 67.6 us; the launch traced here: 67.5 us
  Pallas kernels  64.5 us (95%)
  between operations  1.8 us (3%)
  local copies, waits for them, and re-layouts  1.23 us (2%)
    pallas_call x1, Pallas kernels, local_prog(): pl.pallas_call(kernel, out_shape=(pltpu.VMEM((dim, half), BF16), pltpu.VM...  64.5 us

profile of v5, /device:TPU:1, one launch (start us, length us, event | category | flops | bytes accessed | tf_op | source)
XLA Modules:
  0.0 67.5 jit_solution(10546163124744152124)
XLA Ops:
  0.6 64.5 %shard_map.67 = (bf16[64,512]{1,0:T(8,128)(2,1)S(1)}, bf16[32,64]{1,0:T(8,128)(2,1)S(1)}, f32[1,1]{1,0:T(1,128)S(1)}) custom-call(s32[1024,2048]{1,0:T(8,128)} %m_hbm.1, bf16[64,512]{1,0:T(8,128)(2,1)} %bitcast.5, bf16[32,64]{1,0:T(8,128)(2,1)} %ei_hbm.1, s32[3,128]{1,0:T(4,128)} %bitcast.6), custom_call_target="tpu_custom_call" | custom-call | tf_op jit(solution)/shard_map/pallas_call | solution.py:380
  65.2 0.6 copy.10
  65.8 0.6 copy.11

commit v6 on v5

--- a/solution.py
+++ b/solution.py
@@ -21,6 +21,8 @@
 
     offsets = [(dx, dy, dz) for dz in range(side) for dy in range(side) for dx in range(side)]
     offsets = sorted(offsets[1:], key=lambda o: -(far(o[0]) + far(o[1]) + far(o[2])))
+
+    by_axis = sorted(offsets, key=lambda o: (-far(o[2]), -far(o[1]), -far(o[0])))
 
     def kernel(m_hbm, eu_hbm, ei_hbm, trip_hbm, ou_hbm, oi_hbm, loss_hbm,
                m32, a, at, cacc, trip, deg, usum, suc, svr, svc, eu0t, ei0, e0p, e0d, pan1, pan2,
@@ -70,16 +72,14 @@
             pltpu.make_async_copy(ref, ref, sem).wait()
 
         def spread(ref, ssem, rsem):
-            for o in offsets:
+            for o in by_axis:
                 send(ref, ref, ssem, rsem, {"row": peer(o)})
 
         def unpack(src, dst):
-            def body(i, carry):
-                v = src[pl.ds(i * plane, plane)].astype(F32)
+            for i in range(rows_n // plane):
+                v = src[i * plane:(i + 1) * plane].astype(F32)
                 both = jnp.concatenate([dup_lo(v), dup_hi(v)], axis=1).astype(BF16)
-                dst[pl.ds(pl.multiple_of(i * plane * shard, plane * shard), plane * shard), :] = both.reshape(plane * shard, LANES)
-                return carry
-            lax.fori_loop(0, rows_n // plane, body, 0)
+                dst[i * plane * shard:(i + 1) * plane * shard, :] = both.reshape(plane * shard, LANES)
 
         def stack(v, w, k):
             n = v.shape[0]
@@ -188,6 +188,14 @@
                         send(q.at[o[0] + side * o[1] + plane * o[2]], r.at[me], ssem, rsem, {"row": peer(o)})
             r[me] = q[0]
 
+        def item_sums_late(w, q, r, ssem, rsem):
+            for dz in range(side):
+                v = jnp.dot(at[dz * plane * hs:(dz + 1) * plane * hs, :], w[...], preferred_element_type=F32)
+                q[dz * plane:(dz + 1) * plane] = v.reshape(plane, hs, LANES)
+            for o in by_axis:
+                send(q.at[o[0] + side * o[1] + plane * o[2]], r.at[me], ssem, rsem, {"row": peer(o)})
+            r[me] = q[0]
+
         def axis_view(ref, axis, d, part):
             return (ref.at[:, :, d, part], ref.at[:, d, :, part], ref.at[d, :, :, part])[axis]
 
@@ -246,7 +254,7 @@
                 if w is not None:
                     stack(s, w, k)
 
-        item_sums(w0, q1, r1, r1_s, r1_r)
+        item_sums_late(w0, q1, r1, r1_s, r1_r)
 
         def scale_a(b, carry):
             r = pl.ds(pl.multiple_of(b * LANES, LANES), LANES)

time: 67.6 us -> 66.5 us (0.984)
  Pallas kernels: 64.5 us -> 63.3 us
    pallas_call x1, Pallas kernels: 64.5 us -> 63.3 us  [local_prog(): pl.pallas_call(kernel, out_shape=(pltpu.VMEM((dim, half), BF16), pltpu.VM...]
where the time goes in v6:
time: 66.5 us; the launch traced here: 66.4 us
  Pallas kernels  63.3 us (95%)
  between operations  1.8 us (3%)
  local copies, waits for them, and re-layouts  1.23 us (2%)
    pallas_call x1, Pallas kernels, local_prog(): pl.pallas_call(kernel, out_shape=(pltpu.VMEM((dim, half), BF16), pltpu.VM...  63.3 us

profile of v6, /device:TPU:1, one launch (start us, length us, event | category | flops | bytes accessed | tf_op | source)
XLA Modules:
  0.0 66.4 jit_solution(7490938183835193851)
XLA Ops:
  0.6 63.3 %shard_map.67 = (bf16[64,512]{1,0:T(8,128)(2,1)S(1)}, bf16[32,64]{1,0:T(8,128)(2,1)S(1)}, f32[1,1]{1,0:T(1,128)S(1)}) custom-call(s32[1024,2048]{1,0:T(8,128)} %m_hbm.1, bf16[64,512]{1,0:T(8,128)(2,1)} %bitcast.5, bf16[32,64]{1,0:T(8,128)(2,1)} %ei_hbm.1, s32[3,128]{1,0:T(4,128)} %bitcast.6), custom_call_target="tpu_custom_call" | custom-call | tf_op jit(solution)/shard_map/pallas_call | solution.py:388
  64.0 0.6 copy.10
  64.7 0.6 copy.11

commit v7 on v6

--- a/solution.py
+++ b/solution.py
@@ -183,7 +183,7 @@
             for dz in sorted(range(side), key=lambda d: -far(d)):
                 v = jnp.dot(at[dz * plane * hs:(dz + 1) * plane * hs, :], w[...], preferred_element_type=F32)
                 q[dz * plane:(dz + 1) * plane] = v.reshape(plane, hs, LANES)
-                for o in offsets:
+                for o in by_axis:
                     if o[2] == dz:
                         send(q.at[o[0] + side * o[1] + plane * o[2]], r.at[me], ssem, rsem, {"row": peer(o)})
             r[me] = q[0]

time: 66.5 us -> 66.3 us (level)
  no operation moved by 1% of the time
where the time goes in v7:
time: 66.3 us; the launch traced here: 66.2 us
  Pallas kernels  63.1 us (95%)
  between operations  1.8 us (3%)
  local copies, waits for them, and re-layouts  1.23 us (2%)
    pallas_call x1, Pallas kernels, local_prog(): pl.pallas_call(kernel, out_shape=(pltpu.VMEM((dim, half), BF16), pltpu.VM...  63.1 us

profile of v7, /device:TPU:1, one launch (start us, length us, event | category | flops | bytes accessed | tf_op | source)
XLA Modules:
  0.0 66.2 jit_solution(11449925730137711980)
XLA Ops:
  0.6 63.1 %shard_map.67 = (bf16[64,512]{1,0:T(8,128)(2,1)S(1)}, bf16[32,64]{1,0:T(8,128)(2,1)S(1)}, f32[1,1]{1,0:T(1,128)S(1)}) custom-call(s32[1024,2048]{1,0:T(8,128)} %m_hbm.1, bf16[64,512]{1,0:T(8,128)(2,1)} %bitcast.5, bf16[32,64]{1,0:T(8,128)(2,1)} %ei_hbm.1, s32[3,128]{1,0:T(4,128)} %bitcast.6), custom_call_target="tpu_custom_call" | custom-call | tf_op jit(solution)/shard_map/pallas_call | solution.py:388
  63.8 0.6 copy.10
  64.5 0.6 copy.11
